TPU v7x, 512 devices: a 8x2x16 block of a 8x8x16 slice. The times are simulated.
512 devices in a mesh: groups: 2 (over y), docs: 16 (over z), mp: 8 (over x), sub: 2 (over core).
Axes of the slice: x: 8, y: 2, z: 16, core: 2. Of those that a mesh axis runs over, the one named last changes fastest.
The devices are a block of a 8x8x16 slice.
Arguments:
- embeddings: bfloat16 [65536, 1024], P(('groups', 'docs', 'mp', 'sub')), parts along dimension 0, may hold values from -6 to 6
- owner_shard: int32 [65536, 1], P(('groups', 'docs', 'mp', 'sub')), parts along dimension 0, may hold values from 0 to 15; in each aligned block of 128 rows (0 to 127, 128 to 255, ...) at most 16 rows name the same one
- query_local: int32 [65536], P(('groups', 'docs', 'mp', 'sub')), parts along dimension 0, may hold values from 0 to 1
- labels: int32 [65536], P(('groups', 'docs', 'mp', 'sub')), parts along dimension 0, may hold values from 0 to 4
- w_first: bfloat16 [1024, 1024], replicated, may hold values from -0.1875 to 0.1875
- w_second: float32 [1024], replicated, may hold values from -0.1875 to 0.1875
Outputs:
- emb_grad: bfloat16 [65536, 1024], P(('groups', 'docs', 'mp', 'sub')), parts along dimension 0
- w_first_grad: float32 [2048, 1024], P(('groups', 'mp', 'sub')), parts along dimension 0
- w_second_grad: float32 [2048], P('groups'), parts along dimension 0
There are 2 independent parts, one for each index of `groups`. A program takes and returns all parts, laid end to end along the dimension named above; an argument that names none is the same for every part. Nothing has to cross between parts.
Inputs may be any that keep to these rules, and one draw needn't show every extreme that they name: `owner_shard`: among the 128 rows of one document shard no owner appears more than 16 times, and some owner appears exactly 16 times.
All inputs are finite; a program needn't handle non-finite values.
Results may differ from a plain program's by a relative error of at most 0.017.
Values may be sent and summed in bfloat16 or wider, within the bound.
No kernel may reach another device: no remote copies, remote signals or barrier semaphores. Data moves between devices by JAX's collectives and lax.ppermute only.
A program may use at most 64 MiB of HBM per device.

v0:
```python
import functools

import jax
import jax.numpy as jnp
from jax import lax
from jax.experimental import pallas as pl
from jax.experimental.pallas import tpu as pltpu
from jax.sharding import PartitionSpec as P


LANES = 128


def whole(*shape_and_type):
    return jax.ShapeDtypeStruct(*shape_and_type)


def vmem_specs(count):
    return [pl.BlockSpec(memory_space=pltpu.VMEM)] * count


def score_kernel(capacity, emb_ref, w1_ref, w2_ref, owner_ref, query_ref, label_ref, sent_ref, slot_ref):
    rows = emb_ref.shape[0]
    halves = sent_ref.shape[1] // 4
    along = lax.broadcasted_iota(jnp.int32, (rows, rows), 1)
    down = lax.broadcasted_iota(jnp.int32, (rows, rows), 0)

    def column(row):
        return jnp.sum(jnp.where(along == down, row, 0), axis=1, keepdims=True)

    owner = owner_ref[...]
    owner_column = column(owner)
    earlier = jnp.where((owner_column == owner) & (along < down), 1, 0)
    slot = owner_column * capacity + jnp.sum(earlier, axis=1, keepdims=True)
    slot_ref[...] = slot
    mark = column(query_ref[...] + 1).astype(jnp.float32)
    label = column(label_ref[...]).astype(jnp.float32)

    pre_act = jnp.dot(emb_ref[...], w1_ref[...], preferred_element_type=jnp.float32)
    hidden = pre_act * jax.nn.sigmoid(pre_act)
    score = jnp.sum(hidden * w2_ref[...], axis=1, keepdims=True)

    lane = lax.broadcasted_iota(jnp.int32, (rows, LANES), 1)
    sent_ref[...] = jnp.zeros_like(sent_ref)
    for h in range(halves):
        here = slot == lane + h * LANES
        for place, value in enumerate((score, mark, label)):
            row = jnp.sum(jnp.where(here, value, 0.0), axis=0, keepdims=True)
            for target in range(sent_ref.shape[0]):
                sent_ref[target, place * halves + h : place * halves + h + 1, :] = row


def within_groups(x, capacity):
    lane = lax.broadcasted_iota(jnp.int32, x.shape, 1)
    out = [x]
    step = capacity // 2
    while step:
        upper = (lane & step) != 0
        spread = []
        for y in out:
            spread.append(jnp.where(upper, pltpu.roll(y, step, 1), y))
            spread.append(jnp.where(upper, y, pltpu.roll(y, LANES - step, 1)))
        out = spread
        step //= 2
    return out


def group_sum(x, capacity):
    lane = lax.broadcasted_iota(jnp.int32, x.shape, 1)
    step = capacity // 2
    while step:
        upper = (lane & step) != 0
        x = x + jnp.where(upper, pltpu.roll(x, step, 1), pltpu.roll(x, LANES - step, 1))
        step //= 2
    return x


def lambda_kernel(
    capacity, place_ref, got_ref, slot_ref, spread_ref, column_ref,
    score_by, mark_by, key_by, disc_by, row_scratch,
):
    sources = got_ref.shape[0]
    halves = got_ref.shape[1] // 4
    me = place_ref[0]
    rows = slot_ref.shape[0]
    source = lax.broadcasted_iota(jnp.int32, (sources, LANES), 0)
    lane = lax.broadcasted_iota(jnp.int32, (sources, LANES), 1)
    position = (source * capacity + lane % capacity).astype(jnp.float32)
    slots = float(sources * capacity)
    lane_of_row = lax.broadcasted_iota(jnp.int32, (rows, LANES), 1)
    lambda_column = jnp.zeros((rows, 1), jnp.float32)
    for h in range(halves):
        half_score = got_ref[:, h, :] * 0.5
        mark = got_ref[:, halves + h, :]
        label = got_ref[:, 2 * halves + h, :]
        key = label * slots - position
        for ref, value in ((score_by, half_score), (mark_by, mark), (key_by, key)):
            for c, spread in enumerate(within_groups(value, capacity)):
                ref[c * sources : (c + 1) * sources, :] = spread

        def rank_step(step, sums):
            soft, ideal = sums
            base = pl.multiple_of(step * 8, 8)
            score_rows = score_by[pl.ds(base, 8), :]
            mark_rows = mark_by[pl.ds(base, 8), :]
            key_rows = key_by[pl.ds(base, 8), :]
            for r in range(8):
                same = mark_rows[r : r + 1, :] == mark
                tilt = jnp.tanh(score_rows[r : r + 1, :] - half_score)
                soft = soft + jnp.where(same, tilt + 1.0, 0.0)
                ideal = ideal + jnp.where(same & (key_rows[r : r + 1, :] > key), 1.0, 0.0)
            return soft, ideal

        nothing = jnp.zeros((sources, LANES), jnp.float32)
        soft, ideal = lax.fori_loop(0, capacity * sources // 8, rank_step, (nothing, nothing))
        discount = 1.0 / jnp.log2(2.0 + (0.5 * soft - 0.5))
        gain = jnp.exp2(label) - 1.0
        term = gain / jnp.log2(2.0 + ideal)
        for c, spread in enumerate(within_groups(discount, capacity)):
            disc_by[c * sources : (c + 1) * sources, :] = spread

        for place, value in enumerate((half_score, mark, gain, discount)):
            row_scratch[place * sources : (place + 1) * sources, :] = value
        own_score, own_mark, own_gain, own_disc = (
            row_scratch[pl.ds(place * sources + me, 1), :] for place in range(4)
        )
        ideal_sum = jnp.zeros((1, LANES), jnp.float32)
        for query in range(2):
            asked = query + 1.0
            per_lane = jnp.sum(jnp.where(mark == asked, term, 0.0), axis=0, keepdims=True)
            spread = group_sum(jnp.broadcast_to(per_lane, (8, LANES)), capacity)[:1, :]
            ideal_sum = jnp.where(own_mark == asked, spread, ideal_sum)
        inv_ideal = jnp.where(ideal_sum > 0.0, 1.0 / jnp.where(ideal_sum > 0.0, ideal_sum, 1.0), 0.0)

        total = jnp.zeros((sources, LANES), jnp.float32)
        for c in range(capacity):
            at = slice(c * sources, (c + 1) * sources)
            their_gain = jnp.exp2(jnp.ceil(key_by[at, :] * (1.0 / slots))) - 1.0
            gain_gap = own_gain - their_gain
            gap = 2.0 * (score_by[at, :] - own_score)
            pull = jax.nn.sigmoid(jnp.where(gain_gap > 0.0, gap, -gap))
            pair = -gain_gap * jnp.abs(own_disc - disc_by[at, :]) * pull
            total = total + jnp.where(mark_by[at, :] == own_mark, pair, 0.0)
        lambda_row = jnp.sum(total, axis=0, keepdims=True) * inv_ideal
        here = slot_ref[...] == lane_of_row + h * LANES
        lambda_column = lambda_column + jnp.sum(
            jnp.where(here, lambda_row, 0.0), axis=1, keepdims=True
        )

    column_ref[...] = lambda_column
    along = lax.broadcasted_iota(jnp.int32, (rows, rows), 1)
    down = lax.broadcasted_iota(jnp.int32, (rows, rows), 0)
    row = jnp.sum(jnp.where(along == down, lambda_column, 0.0), axis=0, keepdims=True)
    spread_ref[...] = jnp.broadcast_to(row[None], spread_ref.shape)


def slope_kernel(count, place_ref, w1_ref, w2_ref, *refs):
    emb_refs, (slope_ref, hidden_ref, part_ref) = refs[:count], refs[count:]
    wide = part_ref.shape[2]
    mine = pl.ds(pl.multiple_of(place_ref[1] // 2 * wide, LANES), wide)
    for i, emb_ref in enumerate(emb_refs):
        pre_act = jnp.dot(emb_ref[...], w1_ref[...], preferred_element_type=jnp.float32)
        gate = jax.nn.sigmoid(pre_act)
        hidden_ref[i] = (pre_act * gate).astype(jnp.bfloat16)
        slope = gate * (1.0 + pre_act * (1.0 - gate))
        slope_ref[i] = (w2_ref[...] * slope).astype(jnp.bfloat16)
        part_ref[i] = emb_ref[:, mine]


def slopes(place, w_first, w2_row, blocks, wide):
    rows, units = blocks[0].shape[0], w_first.shape[1]
    count = len(blocks)
    return pl.pallas_call(
        functools.partial(slope_kernel, count),
        out_shape=(
            whole((count, rows, units), jnp.bfloat16),
            whole((count, rows, units), jnp.bfloat16),
            whole((count, rows, wide), jnp.bfloat16),
        ),
        in_specs=[pl.BlockSpec(memory_space=pltpu.SMEM)] + vmem_specs(2 + count),
        out_specs=tuple(vmem_specs(3)),
        name="slopes",
    )(place, w_first, w2_row, *blocks)


def product_kernel(groups, place_ref, lambda_ref, *refs):
    inputs, sent_ref = refs[: 3 * len(groups)], refs[-1]
    members, rows = lambda_ref.shape[0], lambda_ref.shape[2]
    my_member = place_ref[1] // 2
    along = lax.broadcasted_iota(jnp.int32, (rows, rows), 1)
    down = lax.broadcasted_iota(jnp.int32, (rows, rows), 0)
    total, second = None, None
    for g, offsets in enumerate(groups):
        slope_ref, hidden_ref, part_ref = inputs[3 * g : 3 * g + 3]
        for i, offset in enumerate(offsets):
            block = lambda_ref[lax.rem(my_member + offset, members)]
            column = jnp.sum(jnp.where(along == down, block[:1], 0.0), axis=1, keepdims=True)
            part = (part_ref[i].astype(jnp.float32) * column).astype(jnp.bfloat16)
            product = lax.dot_general(
                part, slope_ref[i], (((0,), (0,)), ((), ())), preferred_element_type=jnp.float32
            )
            high = block.astype(jnp.bfloat16)
            low = (block - high.astype(jnp.float32)).astype(jnp.bfloat16)
            hidden = hidden_ref[i]
            summed = jnp.dot(high, hidden, preferred_element_type=jnp.float32) + jnp.dot(
                low, hidden, preferred_element_type=jnp.float32
            )
            total = product if total is None else total + product
            second = summed if second is None else second + summed
    targets = sent_ref.shape[0]
    part_rows = total.shape[0] // targets
    columns = total.shape[1] // LANES
    rounded, second = total.astype(jnp.bfloat16), second.astype(jnp.bfloat16)
    for target in range(targets):
        for k in range(columns):
            at = slice(k * LANES, (k + 1) * LANES)
            sent_ref[target, k * part_rows : (k + 1) * part_rows, :] = rounded[
                target * part_rows : (target + 1) * part_rows, at
            ]
            row = part_rows * columns + k
            sent_ref[target, row : row + 1, :] = second[:1, at]


def sent_to_all(x, axis):
    count = lax.axis_size(axis)
    return lax.all_to_all(jnp.broadcast_to(x[None], (count, *x.shape)), axis, 0, 0, tiled=True)


def parity_blocks(block):
    lanes, subs = lax.axis_size("mp"), lax.axis_size("sub")

    def moved(x, by):
        return lax.ppermute(x, "mp", [(i, (i + by) % lanes) for i in range(lanes)])

    back, on = moved(block, 2), moved(block, -2)
    both_ways = [
        (i * subs + s, (i + (2 if s == 0 else -2)) % lanes * subs + s)
        for i in range(lanes)
        for s in range(subs)
    ]
    passed = jnp.where(lax.axis_index("sub") == 0, back, on)
    across = lax.ppermute(passed, ("mp", "sub"), both_ways)
    return back, on, across


def on_device(embeddings, owner_shard, query_local, labels, w_first, w_second):
    docs, lanes, subs = (lax.axis_size(axis) for axis in ("docs", "mp", "sub"))
    rows, width = embeddings.shape
    units = w_first.shape[1]
    capacity = 2 * rows // docs
    halves = docs * capacity // LANES
    w2_row = w_second.reshape(1, units)
    place = jnp.stack([lax.axis_index(axis) for axis in ("docs", "mp", "sub")]).astype(jnp.int32)
    back, on, across = parity_blocks(embeddings)
    members = lanes // 2
    sent, slot = pl.pallas_call(
        functools.partial(score_kernel, capacity),
        out_shape=(
            whole((docs, 4 * halves, LANES), jnp.float32),
            whole((rows, 1), jnp.int32),
        ),
        in_specs=vmem_specs(6),
        out_specs=tuple(vmem_specs(2)),
        name="score",
    )(
        embeddings, w_first, w2_row,
        owner_shard.reshape(1, rows), query_local.reshape(1, rows), labels.reshape(1, rows),
    )
    got = lax.all_to_all(sent, "docs", 0, 0, tiled=True)
    spread, lambda_column = pl.pallas_call(
        functools.partial(lambda_kernel, capacity),
        out_shape=(whole((members, 8, rows), jnp.float32), whole((rows, 1), jnp.float32)),
        in_specs=[pl.BlockSpec(memory_space=pltpu.SMEM)] + vmem_specs(2),
        out_specs=tuple(vmem_specs(2)),
        scratch_shapes=[pltpu.VMEM((docs * capacity, LANES), jnp.float32)] * 4
        + [pltpu.VMEM((4 * docs, LANES), jnp.float32)],
        name="lambdas",
    )(place, got, slot)
    parities = [list(range(parity, lanes, 2)) for parity in range(2)]
    all_lambdas = lax.all_to_all(
        spread, "mp", 0, 0, axis_index_groups=parities, tiled=True
    )

    part_rows = width // (lanes * subs)
    targets = 2 * subs
    wide = targets * part_rows
    columns = units // LANES
    own = slopes(place, w_first, w2_row, [embeddings], wide)
    beside = slopes(place, w_first, w2_row, [back, on], wide)
    beyond = slopes(place, w_first, w2_row, [across], wide)
    own_grad = lax.dot_general(
        own[0][0], w_first, (((1,), (1,)), ((), ())), preferred_element_type=jnp.float32
    )
    emb_grad = (lambda_column * own_grad).astype(jnp.bfloat16)
    all_lambdas, emb_grad = lax.optimization_barrier((all_lambdas, emb_grad))
    offsets = ((0,), (members - 1, 1), (2,))
    sent = pl.pallas_call(
        functools.partial(product_kernel, offsets),
        out_shape=whole((targets, (part_rows + 1) * columns, LANES), jnp.bfloat16),
        in_specs=[pl.BlockSpec(memory_space=pltpu.SMEM)] + vmem_specs(10),
        out_specs=vmem_specs(1)[0],
        name="product",
    )(place, all_lambdas, *own, *beside, *beyond)
    cells = [list(range(i, i + targets)) for i in range(0, lanes * subs, targets)]
    arrived = lax.all_to_all(
        sent, ("mp", "sub"), 0, 0, axis_index_groups=cells, tiled=True
    )
    line_sum = arrived.astype(jnp.float32).sum(axis=0).astype(jnp.bfloat16)
    first_rows = part_rows * columns
    tiles = line_sum[:first_rows].reshape(docs, first_rows // docs, LANES)
    second = jnp.broadcast_to(line_sum[first_rows:][None], (docs, columns, LANES))
    arrived = lax.all_to_all(jnp.concatenate([tiles, second], axis=1), "docs", 0, 0, tiled=True)
    shard_sum = arrived.astype(jnp.float32).sum(axis=0)
    w_second_grad = shard_sum[first_rows // docs :].reshape(units)
    spread = sent_to_all(shard_sum[: first_rows // docs].astype(jnp.bfloat16), "docs")
    w_first_grad = (
        spread.reshape(columns, part_rows, LANES).transpose(1, 0, 2).reshape(part_rows, units)
    ).astype(jnp.float32)
    return (emb_grad, w_first_grad, w_second_grad)


def solution(mesh):
    split = ("groups", "docs", "mp", "sub")
    return jax.shard_map(
        on_device,
        mesh=mesh,
        in_specs=(P(split, None), P(split, None), P(split), P(split), P(), P()),
        out_specs=(P(split, None), P(("groups", "mp", "sub"), None), P("groups")),
        check_vma=False,
    )
```

profile of v0, /device:TPU:80, one launch (start us, length us, event | category | flops | bytes accessed | tf_op | source)
XLA Modules:
  0.0 151.3 jit_solution(13043083628669762547)
XLA Ops:
  0.6 6.5 %collective-permute-start.1 = (bf16[128,1024]{1,0:T(8,128)(2,1)}, bf16[128,1024]{1,0:T(8,128)(2,1)S(1)}, u32[]{:S(2)}, u32[]{:S(2)}) collective-permute-start(bf16[128,1024]{1,0:T(8,128)(2,1)} %refs_0_.1), channel_id=1, source_target_pairs={{0,12},{2,14},{4,0},{6,2},{8,4},{10,6},{12,8},{14,10},{1,13},{3,15... | collective-permute-start | bytes 786440 | tf_op jit(solution)/shard_map/ppermute | solution.py:233
  7.1 2.0 %collective-permute-start = (bf16[128,1024]{1,0:T(8,128)(2,1)}, bf16[128,1024]{1,0:T(8,128)(2,1)S(1)}, u32[]{:S(2)}, u32[]{:S(2)}) collective-permute-start(bf16[128,1024]{1,0:T(8,128)(2,1)} %refs_0_.1), channel_id=1, source_target_pairs={{0,4},{2,6},{4,8},{6,10},{8,12},{10,14},{12,0},{14,2},{1,5},{3,7},... | collective-permute-start | bytes 786440 | tf_op jit(solution)/shard_map/ppermute | solution.py:233
  9.1 2.8 %score.1 = (f32[16,8,128]{2,1,0:T(8,128)}, s32[128,1]{1,0:T(8,128)}) custom-call(bf16[128,1024]{1,0:T(8,128)(2,1)} %refs_0_.1, bf16[1024,1024]{1,0:T(8,128)(2,1)} %w1_ref.7, f32[1,1024]{1,0:T(1,128)} %bitcast.28, s32[1,128]{1,0:T(1,128)} %bitcast.32, s32[1,128]{1,0:T(1,128)} %bitcast.33, s32[1,128]{1,0:T(1,128)} %bitcast.34), custom_call_target="tpu_custom_call" | custom-call | tf_op jit(solution)/shard_map/score/pallas_call | solution.py:256
  11.9 43.8 %all-to-all-start = ((f32[16,8,128]{2,1,0:T(8,128)}), f32[16,8,128]{2,1,0:T(8,128)S(1)}, u32[]{:S(2)}, u32[]{:S(2)}) async-start(f32[16,8,128]{2,1,0:T(8,128)} %get-tuple-element.18), calls=%async_computation | async-start | bytes 131072 | tf_op jit(solution)/shard_map/all_to_all | solution.py:269
  55.7 0.6 pad_add_fusion.place_ref
  56.3 2.9 %slopes.3 = (bf16[1,128,1024]{2,1,0:T(8,128)(2,1)}, bf16[1,128,1024]{2,1,0:T(8,128)(2,1)}, bf16[1,128,256]{2,1,0:T(8,128)(2,1)}) custom-call(s32[3]{0:T(128)} %pad_add_fusion.place_ref, bf16[1024,1024]{1,0:T(8,128)(2,1)} %w1_ref.7, f32[1,1024]{1,0:T(1,128)} %bitcast.29, bf16[128,1024]{1,0:T(8,128)(2,1)} %refs_0_.1), custom_call_target="tpu_custom_call" | custom-call | tf_op jit(solution)/shard_map/slopes/pallas_call | solution.py:173
  59.2 9.0 %all-to-all-done.got_ref = f32[16,8,128]{2,1,0:T(8,128)S(1)} async-done(((f32[16,8,128]{2,1,0:T(8,128)}), f32[16,8,128]{2,1,0:T(8,128)S(1)}, u32[]{:S(2)}, u32[]{:S(2)}) %all-to-all-start) | async-done | bytes 65568 | tf_op jit(solution)/shard_map/all_to_all | solution.py:269
  68.3 0.6 copy-done.3
  68.9 4.7 %lambdas.1 = (f32[4,8,128]{2,1,0:T(8,128)}, f32[128,1]{1,0:T(8,128)}) custom-call(s32[3]{0:T(128)} %pad_add_fusion.place_ref, f32[16,8,128]{2,1,0:T(8,128)} %copy-done.3, s32[128,1]{1,0:T(8,128)} %get-tuple-element.19.slot_ref), custom_call_target="tpu_custom_call" | custom-call | tf_op jit(solution)/shard_map/lambdas/pallas_call | solution.py:270
  73.6 5.8 %all-to-all-start.1 = ((f32[4,8,128]{2,1,0:T(8,128)}), f32[4,8,128]{2,1,0:T(8,128)S(1)}, u32[]{:S(2)}, u32[]{:S(2)}) async-start(f32[4,8,128]{2,1,0:T(8,128)} %get-tuple-element.20), calls=%async_computation.1 | async-start | bytes 32768 | tf_op jit(solution)/shard_map/all_to_all | solution.py:280
  79.4 0.9 reduce.1
  80.4 4.9 %collective-permute-start.2 = (bf16[128,1024]{1,0:T(8,128)(2,1)S(1)}, bf16[128,1024]{1,0:T(8,128)(2,1)S(1)}, u32[]{:S(2)}, u32[]{:S(2)}) collective-permute-start(bf16[128,1024]{1,0:T(8,128)(2,1)S(1)} %broadcast_select_fusion), channel_id=1, source_target_pairs={{0,4},{1,13},{2,6},{3,15},{4,8},{5,1},{6,10},{7,3},{8,12},{9,5},{1... | collective-permute-start | bytes 786440 | tf_op jit(solution)/shard_map/ppermute | solution.py:242
  85.3 2.5 %fusion = bf16[128,1024]{1,0:T(8,128)(2,1)} fusion(bf16[1024,1024]{1,0:T(8,128)(2,1)S(1)} %copy-done, bf16[1,128,1024]{2,1,0:T(8,128)(2,1)} %get-tuple-element.22.refs_0_, f32[128]{0:T(128)S(1)} %reduce.1), kind=kOutput, calls=%fused_computation.1 | convolution fusion | flops 268697600 | bytes 2621952 | tf_op jit(solution)/shard_map/dot_general | solution.py:291
  87.8 3.6 %slopes.4 = (bf16[2,128,1024]{2,1,0:T(8,128)(2,1)}, bf16[2,128,1024]{2,1,0:T(8,128)(2,1)}, bf16[2,128,256]{2,1,0:T(8,128)(2,1)}) custom-call(s32[3]{0:T(128)} %pad_add_fusion.place_ref, bf16[1024,1024]{1,0:T(8,128)(2,1)} %w1_ref.7, f32[1,1024]{1,0:T(1,128)} %bitcast.30, bf16[128,1024]{1,0:T(8,128)(2,1)} %copy-done.2, bf16[128,1024]{1,0:T(8,128)(2,1)} %copy-done.1), custom_call_target="tpu_custom_call" | custom-call | tf_op jit(solution)/shard_map/slopes/pallas_call | solution.py:173
  91.7 0.7 copy-done.4
  92.4 3.0 %slopes.5 = (bf16[1,128,1024]{2,1,0:T(8,128)(2,1)}, bf16[1,128,1024]{2,1,0:T(8,128)(2,1)}, bf16[1,128,256]{2,1,0:T(8,128)(2,1)}) custom-call(s32[3]{0:T(128)} %pad_add_fusion.place_ref, bf16[1024,1024]{1,0:T(8,128)(2,1)} %w1_ref.7, f32[1,1024]{1,0:T(1,128)} %bitcast.31, bf16[128,1024]{1,0:T(8,128)(2,1)} %copy-done.4), custom_call_target="tpu_custom_call" | custom-call | tf_op jit(solution)/shard_map/slopes/pallas_call | solution.py:173
  95.4 3.4 %product.1 = bf16[4,520,128]{2,1,0:T(8,128)(2,1)} custom-call(s32[3]{0:T(128)} %pad_add_fusion.place_ref, f32[4,8,128]{2,1,0:T(8,128)} %copy-done.5, bf16[1,128,1024]{2,1,0:T(8,128)(2,1)} %get-tuple-element.22.refs_0_, bf16[1,128,1024]{2,1,0:T(8,128)(2,1)} %get-tuple-element.25.refs_1_, bf16[1,128,256]{2,1,0:T(8,128)(2,1)} %get-tuple-element.26.refs_2_, ...), custom_call_target="tpu_custom_call" | custom-call | tf_op jit(solution)/shard_map/product/pallas_call | solution.py:297
  98.8 12.9 %all_to_all.25 = bf16[4,520,128]{2,1,0:T(8,128)(2,1)S(1)} all-to-all(bf16[4,520,128]{2,1,0:T(8,128)(2,1)} %product.1), channel_id=1, replica_groups={{0,1,2,3},{4,5,6,7},{8,9,10,11},{12,13,14,15},{16,17,18,19},{20,21,22,2..., dimensions={0} | all-to-all | bytes 1064960 | tf_op jit(solution)/shard_map/all_to_all | solution.py:305
  111.9 17.8 %all_to_all.26 = bf16[16,40,128]{2,1,0:T(8,128)(2,1)S(1)} all-to-all(bf16[16,40,128]{2,1,0:T(8,128)(2,1)S(1)} %pad_maximum_fusion), channel_id=1, replica_groups=mesh['groups'=2,'docs'=16,'mp'=8,'sub'=2] {'docs'}, dimensions={0} | all-to-all | bytes 327680 | tf_op jit(solution)/shard_map/all_to_all | solution.py:312
  129.8 0.7 broadcast_in_dim.5
  130.5 5.5 %all-to-all-start.4 = ((bf16[16,32,128]{2,1,0:T(8,128)(2,1)}), bf16[16,32,128]{2,1,0:T(8,128)(2,1)S(1)}, u32[]{:S(2)}, u32[]{:S(2)}) async-start(bf16[16,32,128]{2,1,0:T(8,128)(2,1)} %broadcast_in_dim.5), calls=%async_computation.4 | async-start | bytes 262144 | tf_op jit(solution)/shard_map/all_to_all | solution.py:226
  136.0 0.6 slice_bitcast_fusion
  136.6 14.0 %all-to-all-done.4 = bf16[16,32,128]{2,1,0:T(8,128)(2,1)S(1)} async-done(((bf16[16,32,128]{2,1,0:T(8,128)(2,1)}), bf16[16,32,128]{2,1,0:T(8,128)(2,1)S(1)}, u32[]{:S(2)}, u32[]{:S(2)}) %all-to-all-start.4) | async-done | bytes 131104 | tf_op jit(solution)/shard_map/all_to_all | solution.py:226
  150.6 0.7 copy_bitcast_fusion
  (22 shorter events, 0.5 us)
Async XLA Ops:
  0.6 79.7 %collective-permute-start.1 = (bf16[128,1024]{1,0:T(8,128)(2,1)}, bf16[128,1024]{1,0:T(8,128)(2,1)S(1)}, u32[]{:S(2)}, u32[]{:S(2)}) collective-permute-start(bf16[128,1024]{1,0:T(8,128)(2,1)} %refs_0_.1), channel_id=1, source_target_pairs={{0,12},{2,14},{4,0},{6,2},{8,4},{10,6},{12,8},{14,10},{1,13},{3,15... | collective-permute-start | bytes 786440 | tf_op jit(solution)/shard_map/ppermute | solution.py:233
  7.1 73.2 %collective-permute-start = (bf16[128,1024]{1,0:T(8,128)(2,1)}, bf16[128,1024]{1,0:T(8,128)(2,1)S(1)}, u32[]{:S(2)}, u32[]{:S(2)}) collective-permute-start(bf16[128,1024]{1,0:T(8,128)(2,1)} %refs_0_.1), channel_id=1, source_target_pairs={{0,4},{2,6},{4,8},{6,10},{8,12},{10,14},{12,0},{14,2},{1,5},{3,7},... | collective-permute-start | bytes 786440 | tf_op jit(solution)/shard_map/ppermute | solution.py:233
  11.9 73.4 %copy-start = (bf16[1024,1024]{1,0:T(8,128)(2,1)S(1)}, bf16[1024,1024]{1,0:T(8,128)(2,1)}, u32[]{:S(2)}) copy-start(bf16[1024,1024]{1,0:T(8,128)(2,1)} %w1_ref.7) | copy-start | bytes 6291460
  11.9 56.4 %all-to-all-start = ((f32[16,8,128]{2,1,0:T(8,128)}), f32[16,8,128]{2,1,0:T(8,128)S(1)}, u32[]{:S(2)}, u32[]{:S(2)}) async-start(f32[16,8,128]{2,1,0:T(8,128)} %get-tuple-element.18), calls=%async_computation | async-start | bytes 131072 | tf_op jit(solution)/shard_map/all_to_all | solution.py:269
  68.3 0.6 copy-start.3
  73.6 17.8 %all-to-all-start.1 = ((f32[4,8,128]{2,1,0:T(8,128)}), f32[4,8,128]{2,1,0:T(8,128)S(1)}, u32[]{:S(2)}, u32[]{:S(2)}) async-start(f32[4,8,128]{2,1,0:T(8,128)} %get-tuple-element.20), calls=%async_computation.1 | async-start | bytes 32768 | tf_op jit(solution)/shard_map/all_to_all | solution.py:280
  80.4 7.4 %copy-start.1 = (bf16[128,1024]{1,0:T(8,128)(2,1)}, bf16[128,1024]{1,0:T(8,128)(2,1)S(1)}, u32[]{:S(2)}) copy-start(bf16[128,1024]{1,0:T(8,128)(2,1)S(1)} %collective-permute-done.1.refs_1_) | copy-start | bytes 786436
  80.4 7.4 %copy-start.2 = (bf16[128,1024]{1,0:T(8,128)(2,1)}, bf16[128,1024]{1,0:T(8,128)(2,1)S(1)}, u32[]{:S(2)}) copy-start(bf16[128,1024]{1,0:T(8,128)(2,1)S(1)} %collective-permute-done.refs_0_) | copy-start | bytes 786436
  80.4 11.3 %collective-permute-start.2 = (bf16[128,1024]{1,0:T(8,128)(2,1)S(1)}, bf16[128,1024]{1,0:T(8,128)(2,1)S(1)}, u32[]{:S(2)}, u32[]{:S(2)}) collective-permute-start(bf16[128,1024]{1,0:T(8,128)(2,1)S(1)} %broadcast_select_fusion), channel_id=1, source_target_pairs={{0,4},{1,13},{2,6},{3,15},{4,8},{5,1},{6,10},{7,3},{8,12},{9,5},{1... | collective-permute-start | bytes 786440 | tf_op jit(solution)/shard_map/ppermute | solution.py:242
  91.4 4.0 %copy-start.5 = (f32[4,8,128]{2,1,0:T(8,128)}, f32[4,8,128]{2,1,0:T(8,128)S(1)}, u32[]{:S(2)}) copy-start(f32[4,8,128]{2,1,0:T(8,128)S(1)} %all-to-all-done.1.lambda_ref) | copy-start | bytes 49156
  91.7 0.7 copy-start.4
  130.5 20.1 %all-to-all-start.4 = ((bf16[16,32,128]{2,1,0:T(8,128)(2,1)}), bf16[16,32,128]{2,1,0:T(8,128)(2,1)S(1)}, u32[]{:S(2)}, u32[]{:S(2)}) async-start(bf16[16,32,128]{2,1,0:T(8,128)(2,1)} %broadcast_in_dim.5), calls=%async_computation.4 | async-start | bytes 262144 | tf_op jit(solution)/shard_map/all_to_all | solution.py:226
where the time goes:
time: 152 us; the launch traced here: 151 us
  starting transfers between devices  68.4 us (45%)
  blocking collectives  30.8 us (20%)
  waiting for transfers between devices  23.4 us (15%)
  Pallas kernels  20.5 us (13%)
  local copies, waits for them, and re-layouts  2.64 us (2%)
  matrix products  2.49 us (2%)
  other arithmetic  2.37 us (2%)
    all_to_all x1, starting transfers between devices, on_device(): got = lax.all_to_all(sent, 'docs', 0, 0, tiled=True)  43.8 us
    all_to_all x1, blocking collectives, on_device(): lax.all_to_all(jnp.concatenate([tiles, second], axis=1), 'docs', 0, 0, ti...  17.8 us
    all_to_all x1, waiting for transfers between devices, sent_to_all(): lax.all_to_all(jnp.broadcast_to(x[None], (count, *x.shape)), axis, 0, 0,...  14 us
    all_to_all x1, blocking collectives, on_device(): lax.all_to_all(sent, ('mp', 'sub'), 0, 0, axis_index_groups=cells, tiled=...  12.9 us
    pallas_call x3, Pallas kernels, slopes(): pl.pallas_call(functools.partial(slope_kernel, count), out_shape=(whole((...  9.51 us
    all_to_all x1, waiting for transfers between devices, on_device(): got = lax.all_to_all(sent, 'docs', 0, 0, tiled=True)  9.02 us
    ppermute x2, starting transfers between devices, moved(): return lax.ppermute(x, 'mp', [(i, (i + by) % lanes) for i in range(lanes)])  8.45 us
    all_to_all x1, starting transfers between devices, on_device(): lax.all_to_all(spread, 'mp', 0, 0, axis_index_groups=parities, tiled=True)  5.78 us
  transfers between devices with their start and end apart: 6, of which 3 were waited for; matrix products, arithmetic and copies ran while one was open for 3% of the time, Pallas kernels for 9%

commit v1 on v0

--- a/solution.py
+++ b/solution.py
@@ -285,22 +285,15 @@
     targets = 2 * subs
     wide = targets * part_rows
     columns = units // LANES
-    own = slopes(place, w_first, w2_row, [embeddings], wide)
-    beside = slopes(place, w_first, w2_row, [back, on], wide)
-    beyond = slopes(place, w_first, w2_row, [across], wide)
-    own_grad = lax.dot_general(
-        own[0][0], w_first, (((1,), (1,)), ((), ())), preferred_element_type=jnp.float32
-    )
-    emb_grad = (lambda_column * own_grad).astype(jnp.bfloat16)
-    all_lambdas, emb_grad = lax.optimization_barrier((all_lambdas, emb_grad))
-    offsets = ((0,), (members - 1, 1), (2,))
+    prepared = slopes(place, w_first, w2_row, [embeddings, back, on, across], wide)
+    offsets = ((0, members - 1, 1, 2),)
     sent = pl.pallas_call(
         functools.partial(product_kernel, offsets),
         out_shape=whole((targets, (part_rows + 1) * columns, LANES), jnp.bfloat16),
-        in_specs=[pl.BlockSpec(memory_space=pltpu.SMEM)] + vmem_specs(10),
+        in_specs=[pl.BlockSpec(memory_space=pltpu.SMEM)] + vmem_specs(4),
         out_specs=vmem_specs(1)[0],
         name="product",
-    )(place, all_lambdas, *own, *beside, *beyond)
+    )(place, all_lambdas, *prepared)
     cells = [list(range(i, i + targets)) for i in range(0, lanes * subs, targets)]
     arrived = lax.all_to_all(
         sent, ("mp", "sub"), 0, 0, axis_index_groups=cells, tiled=True
@@ -311,6 +304,11 @@
     second = jnp.broadcast_to(line_sum[first_rows:][None], (docs, columns, LANES))
     arrived = lax.all_to_all(jnp.concatenate([tiles, second], axis=1), "docs", 0, 0, tiled=True)
     shard_sum = arrived.astype(jnp.float32).sum(axis=0)
+    lambda_column, shard_sum = lax.optimization_barrier((lambda_column, shard_sum))
+    own_grad = lax.dot_general(
+        prepared[0][0], w_first, (((1,), (1,)), ((), ())), preferred_element_type=jnp.float32
+    )
+    emb_grad = (lambda_column * own_grad).astype(jnp.bfloat16)
     w_second_grad = shard_sum[first_rows // docs :].reshape(units)
     spread = sent_to_all(shard_sum[: first_rows // docs].astype(jnp.bfloat16), "docs")
     w_first_grad = (

time: 152 us -> 145 us (0.954)
  Pallas kernels: 20.5 us -> 15.8 us
  waiting for transfers between devices: 23.4 us -> 21.5 us
    pallas_call x3 -> x1, Pallas kernels: 9.51 us -> 4.88 us  [slopes(): pl.pallas_call(functools.partial(slope_kernel, count), out_shape=(whole((...]
    all_to_all x1, waiting for transfers between devices: 14 us -> 11.4 us  [sent_to_all(): lax.all_to_all(jnp.broadcast_to(x[None], (count, *x.shape)), axis, 0, 0,...]
    all_to_all x1, waiting for transfers between devices: 0.01 us -> 2.18 us  [on_device(): lax.all_to_all(spread, 'mp', 0, 0, axis_index_groups=parities, tiled=True)]
where the time goes in v1:
time: 145 us; the launch traced here: 144 us
  starting transfers between devices  68.5 us (47%)
  blocking collectives  30.5 us (21%)
  waiting for transfers between devices  21.5 us (15%)
  Pallas kernels  15.8 us (11%)
  local copies, waits for them, and re-layouts  3.23 us (2%)
  matrix products  2.48 us (2%)
  other arithmetic  1.53 us (1%)
    all_to_all x1, starting transfers between devices, on_device(): got = lax.all_to_all(sent, 'docs', 0, 0, tiled=True)  43.7 us
    all_to_all x1, blocking collectives, on_device(): lax.all_to_all(jnp.concatenate([tiles, second], axis=1), 'docs', 0, 0, ti...  17.9 us
    all_to_all x1, blocking collectives, on_device(): lax.all_to_all(sent, ('mp', 'sub'), 0, 0, axis_index_groups=cells, tiled=...  12.5 us
    all_to_all x1, waiting for transfers between devices, sent_to_all(): lax.all_to_all(jnp.broadcast_to(x[None], (count, *x.shape)), axis, 0, 0,...  11.4 us
    ppermute x2, starting transfers between devices, moved(): return lax.ppermute(x, 'mp', [(i, (i + by) % lanes) for i in range(lanes)])  8.45 us
    all_to_all x1, waiting for transfers between devices, on_device(): got = lax.all_to_all(sent, 'docs', 0, 0, tiled=True)  7.9 us
    all_to_all x1, starting transfers between devices, on_device(): lax.all_to_all(spread, 'mp', 0, 0, axis_index_groups=parities, tiled=True)  6.99 us
    all_to_all x1, starting transfers between devices, sent_to_all(): lax.all_to_all(jnp.broadcast_to(x[None], (count, *x.shape)), axis, 0, 0,...  5.41 us
  transfers between devices with their start and end apart: 6, of which 3 were waited for; matrix products, arithmetic and copies ran while one was open for 3% of the time, Pallas kernels for 9%

profile of v1, /device:TPU:80, one launch (start us, length us, event | category | flops | bytes accessed | tf_op | source)
XLA Modules:
  0.0 144.3 jit_solution(13548242814123397813)
XLA Ops:
  0.6 4.6 %collective-permute-start = (bf16[128,1024]{1,0:T(8,128)(2,1)}, bf16[128,1024]{1,0:T(8,128)(2,1)S(1)}, u32[]{:S(2)}, u32[]{:S(2)}) collective-permute-start(bf16[128,1024]{1,0:T(8,128)(2,1)} %refs_0_.1), channel_id=1, source_target_pairs={{0,4},{2,6},{4,8},{6,10},{8,12},{10,14},{12,0},{14,2},{1,5},{3,7},... | collective-permute-start | bytes 786440 | tf_op jit(solution)/shard_map/ppermute | solution.py:233
  5.3 3.8 %collective-permute-start.1 = (bf16[128,1024]{1,0:T(8,128)(2,1)}, bf16[128,1024]{1,0:T(8,128)(2,1)S(1)}, u32[]{:S(2)}, u32[]{:S(2)}) collective-permute-start(bf16[128,1024]{1,0:T(8,128)(2,1)} %refs_0_.1), channel_id=1, source_target_pairs={{0,12},{2,14},{4,0},{6,2},{8,4},{10,6},{12,8},{14,10},{1,13},{3,15... | collective-permute-start | bytes 786440 | tf_op jit(solution)/shard_map/ppermute | solution.py:233
  9.1 2.8 %score.1 = (f32[16,8,128]{2,1,0:T(8,128)}, s32[128,1]{1,0:T(8,128)}) custom-call(bf16[128,1024]{1,0:T(8,128)(2,1)} %refs_0_.1, bf16[1024,1024]{1,0:T(8,128)(2,1)} %w1_ref.3, f32[1,1024]{1,0:T(1,128)} %bitcast.28, s32[1,128]{1,0:T(1,128)} %bitcast.30, s32[1,128]{1,0:T(1,128)} %bitcast.31, s32[1,128]{1,0:T(1,128)} %bitcast.32), custom_call_target="tpu_custom_call" | custom-call | tf_op jit(solution)/shard_map/score/pallas_call | solution.py:256
  11.9 43.7 %all-to-all-start = ((f32[16,8,128]{2,1,0:T(8,128)}), f32[16,8,128]{2,1,0:T(8,128)S(1)}, u32[]{:S(2)}, u32[]{:S(2)}) async-start(f32[16,8,128]{2,1,0:T(8,128)} %get-tuple-element.12), calls=%async_computation | async-start | bytes 131072 | tf_op jit(solution)/shard_map/all_to_all | solution.py:269
  55.7 4.0 %collective-permute-start.2 = (bf16[128,1024]{1,0:T(8,128)(2,1)S(1)}, bf16[128,1024]{1,0:T(8,128)(2,1)S(1)}, u32[]{:S(2)}, u32[]{:S(2)}) collective-permute-start(bf16[128,1024]{1,0:T(8,128)(2,1)S(1)} %broadcast_select_fusion), channel_id=1, source_target_pairs={{0,4},{1,13},{2,6},{3,15},{4,8},{5,1},{6,10},{7,3},{8,12},{9,5},{1... | collective-permute-start | bytes 786440 | tf_op jit(solution)/shard_map/ppermute | solution.py:242
  59.7 0.6 pad_add_fusion.place_ref
  60.2 7.9 %all-to-all-done.got_ref = f32[16,8,128]{2,1,0:T(8,128)S(1)} async-done(((f32[16,8,128]{2,1,0:T(8,128)}), f32[16,8,128]{2,1,0:T(8,128)S(1)}, u32[]{:S(2)}, u32[]{:S(2)}) %all-to-all-start) | async-done | bytes 65568 | tf_op jit(solution)/shard_map/all_to_all | solution.py:269
  68.1 0.6 copy-done.3
  68.7 4.7 %lambdas.1 = (f32[4,8,128]{2,1,0:T(8,128)}, f32[128,1]{1,0:T(8,128)}) custom-call(s32[3]{0:T(128)} %pad_add_fusion.place_ref, f32[16,8,128]{2,1,0:T(8,128)} %copy-done.3, s32[128,1]{1,0:T(8,128)} %get-tuple-element.13.slot_ref), custom_call_target="tpu_custom_call" | custom-call | tf_op jit(solution)/shard_map/lambdas/pallas_call | solution.py:270
  73.4 7.0 %all-to-all-start.1 = ((f32[4,8,128]{2,1,0:T(8,128)}), f32[4,8,128]{2,1,0:T(8,128)S(1)}, u32[]{:S(2)}, u32[]{:S(2)}) async-start(f32[4,8,128]{2,1,0:T(8,128)} %get-tuple-element.15), calls=%async_computation.1 | async-start | bytes 32768 | tf_op jit(solution)/shard_map/all_to_all | solution.py:280
  80.5 0.7 copy-done.4
  81.2 4.9 %slopes.1 = (bf16[4,128,1024]{2,1,0:T(8,128)(2,1)}, bf16[4,128,1024]{2,1,0:T(8,128)(2,1)}, bf16[4,128,256]{2,1,0:T(8,128)(2,1)}) custom-call(s32[3]{0:T(128)} %pad_add_fusion.place_ref, bf16[1024,1024]{1,0:T(8,128)(2,1)} %w1_ref.3, f32[1,1024]{1,0:T(1,128)} %bitcast.29, bf16[128,1024]{1,0:T(8,128)(2,1)} %refs_0_.1, bf16[128,1024]{1,0:T(8,128)(2,1)} %copy-done.1, ...), custom_call_target="tpu_custom_call" | custom-call | tf_op jit(solution)/shard_map/slopes/pallas_call | solution.py:173
  86.0 2.2 %all-to-all-done.1.lambda_ref = f32[4,8,128]{2,1,0:T(8,128)S(1)} async-done(((f32[4,8,128]{2,1,0:T(8,128)}), f32[4,8,128]{2,1,0:T(8,128)S(1)}, u32[]{:S(2)}, u32[]{:S(2)}) %all-to-all-start.1) | async-done | bytes 16416 | tf_op jit(solution)/shard_map/all_to_all | solution.py:280
  88.2 0.6 copy-done.5
  88.8 3.5 %product.1 = bf16[4,520,128]{2,1,0:T(8,128)(2,1)} custom-call(s32[3]{0:T(128)} %pad_add_fusion.place_ref, f32[4,8,128]{2,1,0:T(8,128)} %copy-done.5, bf16[4,128,1024]{2,1,0:T(8,128)(2,1)} %get-tuple-element.16.refs_0_, bf16[4,128,1024]{2,1,0:T(8,128)(2,1)} %get-tuple-element.17.refs_1_, bf16[4,128,256]{2,1,0:T(8,128)(2,1)} %get-tuple-element.18.refs_2_), custom_call_target="tpu_custom_call" | custom-call | tf_op jit(solution)/shard_map/product/pallas_call | solution.py:290
  92.3 12.5 %all_to_all.25 = bf16[4,520,128]{2,1,0:T(8,128)(2,1)S(1)} all-to-all(bf16[4,520,128]{2,1,0:T(8,128)(2,1)} %product.1), channel_id=1, replica_groups={{0,1,2,3},{4,5,6,7},{8,9,10,11},{12,13,14,15},{16,17,18,19},{20,21,22,2..., dimensions={0} | all-to-all | bytes 1064960 | tf_op jit(solution)/shard_map/all_to_all | solution.py:298
  104.9 17.9 %all_to_all.26 = bf16[16,40,128]{2,1,0:T(8,128)(2,1)S(1)} all-to-all(bf16[16,40,128]{2,1,0:T(8,128)(2,1)S(1)} %pad_maximum_fusion), channel_id=1, replica_groups=mesh['groups'=2,'docs'=16,'mp'=8,'sub'=2] {'docs'}, dimensions={0} | all-to-all | bytes 327680 | tf_op jit(solution)/shard_map/all_to_all | solution.py:305
  122.9 0.7 broadcast_in_dim.5
  123.6 5.4 %all-to-all-start.4 = ((bf16[16,32,128]{2,1,0:T(8,128)(2,1)}), bf16[16,32,128]{2,1,0:T(8,128)(2,1)S(1)}, u32[]{:S(2)}, u32[]{:S(2)}) async-start(bf16[16,32,128]{2,1,0:T(8,128)(2,1)} %broadcast_in_dim.5), calls=%async_computation.4 | async-start | bytes 262144 | tf_op jit(solution)/shard_map/all_to_all | solution.py:226
  129.0 0.1 reduce.1
  129.1 0.6 slice_bitcast_fusion
  129.7 2.5 %fusion = bf16[128,1024]{1,0:T(8,128)(2,1)} fusion(bf16[1024,1024]{1,0:T(8,128)(2,1)S(1)} %copy-done, bf16[4,128,1024]{2,1,0:T(8,128)(2,1)} %get-tuple-element.16.refs_0_, f32[128]{0:T(128)S(1)} %reduce.1), kind=kOutput, calls=%fused_computation.1 | convolution fusion | flops 268697600 | bytes 2621952 | tf_op jit(solution)/shard_map/dot_general | solution.py:308
  132.2 11.4 %all-to-all-done.4 = bf16[16,32,128]{2,1,0:T(8,128)(2,1)S(1)} async-done(((bf16[16,32,128]{2,1,0:T(8,128)(2,1)}), bf16[16,32,128]{2,1,0:T(8,128)(2,1)S(1)}, u32[]{:S(2)}, u32[]{:S(2)}) %all-to-all-start.4) | async-done | bytes 131104 | tf_op jit(solution)/shard_map/all_to_all | solution.py:226
  143.6 0.7 copy_bitcast_fusion
  (22 shorter events, 0.2 us)
Async XLA Ops:
  0.6 55.0 %collective-permute-start = (bf16[128,1024]{1,0:T(8,128)(2,1)}, bf16[128,1024]{1,0:T(8,128)(2,1)S(1)}, u32[]{:S(2)}, u32[]{:S(2)}) collective-permute-start(bf16[128,1024]{1,0:T(8,128)(2,1)} %refs_0_.1), channel_id=1, source_target_pairs={{0,4},{2,6},{4,8},{6,10},{8,12},{10,14},{12,0},{14,2},{1,5},{3,7},... | collective-permute-start | bytes 786440 | tf_op jit(solution)/shard_map/ppermute | solution.py:233
  5.3 50.3 %collective-permute-start.1 = (bf16[128,1024]{1,0:T(8,128)(2,1)}, bf16[128,1024]{1,0:T(8,128)(2,1)S(1)}, u32[]{:S(2)}, u32[]{:S(2)}) collective-permute-start(bf16[128,1024]{1,0:T(8,128)(2,1)} %refs_0_.1), channel_id=1, source_target_pairs={{0,12},{2,14},{4,0},{6,2},{8,4},{10,6},{12,8},{14,10},{1,13},{3,15... | collective-permute-start | bytes 786440 | tf_op jit(solution)/shard_map/ppermute | solution.py:233
  11.9 56.2 %all-to-all-start = ((f32[16,8,128]{2,1,0:T(8,128)}), f32[16,8,128]{2,1,0:T(8,128)S(1)}, u32[]{:S(2)}, u32[]{:S(2)}) async-start(f32[16,8,128]{2,1,0:T(8,128)} %get-tuple-element.12), calls=%async_computation | async-start | bytes 131072 | tf_op jit(solution)/shard_map/all_to_all | solution.py:269
  55.6 24.8 %copy-start.1 = (bf16[128,1024]{1,0:T(8,128)(2,1)}, bf16[128,1024]{1,0:T(8,128)(2,1)S(1)}, u32[]{:S(2)}) copy-start(bf16[128,1024]{1,0:T(8,128)(2,1)S(1)} %collective-permute-done.refs_1_) | copy-start | bytes 786436
  55.6 24.8 %copy-start.2 = (bf16[128,1024]{1,0:T(8,128)(2,1)}, bf16[128,1024]{1,0:T(8,128)(2,1)S(1)}, u32[]{:S(2)}) copy-start(bf16[128,1024]{1,0:T(8,128)(2,1)S(1)} %collective-permute-done.1.refs_2_) | copy-start | bytes 786436
  55.7 24.8 %collective-permute-start.2 = (bf16[128,1024]{1,0:T(8,128)(2,1)S(1)}, bf16[128,1024]{1,0:T(8,128)(2,1)S(1)}, u32[]{:S(2)}, u32[]{:S(2)}) collective-permute-start(bf16[128,1024]{1,0:T(8,128)(2,1)S(1)} %broadcast_select_fusion), channel_id=1, source_target_pairs={{0,4},{1,13},{2,6},{3,15},{4,8},{5,1},{6,10},{7,3},{8,12},{9,5},{1... | collective-permute-start | bytes 786440 | tf_op jit(solution)/shard_map/ppermute | solution.py:242
  68.1 0.6 copy-start.3
  73.4 14.8 %all-to-all-start.1 = ((f32[4,8,128]{2,1,0:T(8,128)}), f32[4,8,128]{2,1,0:T(8,128)S(1)}, u32[]{:S(2)}, u32[]{:S(2)}) async-start(f32[4,8,128]{2,1,0:T(8,128)} %get-tuple-element.15), calls=%async_computation.1 | async-start | bytes 32768 | tf_op jit(solution)/shard_map/all_to_all | solution.py:280
  80.5 0.7 copy-start.4
  88.2 0.6 copy-start.5
  92.3 36.7 %copy-start.6 = (f32[128,1]{1,0:T(8,128)S(1)}, f32[128,1]{1,0:T(8,128)}, u32[]{:S(2)}) copy-start(f32[128,1]{1,0:T(8,128)} %get-tuple-element.19) | copy-start | bytes 1540
  92.3 37.5 %copy-start = (bf16[1024,1024]{1,0:T(8,128)(2,1)S(1)}, bf16[1024,1024]{1,0:T(8,128)(2,1)}, u32[]{:S(2)}) copy-start(bf16[1024,1024]{1,0:T(8,128)(2,1)} %w1_ref.3) | copy-start | bytes 6291460
  123.6 20.0 %all-to-all-start.4 = ((bf16[16,32,128]{2,1,0:T(8,128)(2,1)}), bf16[16,32,128]{2,1,0:T(8,128)(2,1)S(1)}, u32[]{:S(2)}, u32[]{:S(2)}) async-start(bf16[16,32,128]{2,1,0:T(8,128)(2,1)} %broadcast_in_dim.5), calls=%async_computation.4 | async-start | bytes 262144 | tf_op jit(solution)/shard_map/all_to_all | solution.py:226

commit v2 on v1

--- a/solution.py
+++ b/solution.py
@@ -221,9 +221,10 @@
             sent_ref[target, row : row + 1, :] = second[:1, at]
 
 
-def sent_to_all(x, axis):
-    count = lax.axis_size(axis)
-    return lax.all_to_all(jnp.broadcast_to(x[None], (count, *x.shape)), axis, 0, 0, tiled=True)
+def docs_exchange(x):
+    count = lax.axis_size("docs")
+    members = [(i + count // 2) % count for i in range(count)]
+    return lax.all_to_all(x, "docs", 0, 0, axis_index_groups=[members], tiled=True)
 
 
 def parity_blocks(block):
@@ -302,7 +303,7 @@
     first_rows = part_rows * columns
     tiles = line_sum[:first_rows].reshape(docs, first_rows // docs, LANES)
     second = jnp.broadcast_to(line_sum[first_rows:][None], (docs, columns, LANES))
-    arrived = lax.all_to_all(jnp.concatenate([tiles, second], axis=1), "docs", 0, 0, tiled=True)
+    arrived = docs_exchange(jnp.concatenate([tiles, second], axis=1))
     shard_sum = arrived.astype(jnp.float32).sum(axis=0)
     lambda_column, shard_sum = lax.optimization_barrier((lambda_column, shard_sum))
     own_grad = lax.dot_general(
@@ -310,7 +311,8 @@
     )
     emb_grad = (lambda_column * own_grad).astype(jnp.bfloat16)
     w_second_grad = shard_sum[first_rows // docs :].reshape(units)
-    spread = sent_to_all(shard_sum[: first_rows // docs].astype(jnp.bfloat16), "docs")
+    mine = shard_sum[: first_rows // docs].astype(jnp.bfloat16)
+    spread = docs_exchange(jnp.broadcast_to(mine[None], (docs, *mine.shape)))
     w_first_grad = (
         spread.reshape(columns, part_rows, LANES).transpose(1, 0, 2).reshape(part_rows, units)
     ).astype(jnp.float32)

time: 145 us -> 146 us (level)
  waiting for transfers between devices: 21.5 us -> 13.4 us
  starting transfers between devices: 68.5 us -> 75.1 us
  blocking collectives: 30.5 us -> 32.5 us
    all_to_all x1, waiting for transfers between devices: 11.4 us -> 3.36 us  [docs_exchange(): lax.all_to_all(x, 'docs', 0, 0, axis_index_groups=[members], tiled=True)]
    all_to_all x1, starting transfers between devices: 5.41 us -> 12 us  [docs_exchange(): lax.all_to_all(x, 'docs', 0, 0, axis_index_groups=[members], tiled=True)]
    all_to_all x1, blocking collectives: 17.9 us -> 20 us  [docs_exchange(): lax.all_to_all(x, 'docs', 0, 0, axis_index_groups=[members], tiled=True)]
where the time goes in v2:
time: 146 us; the launch traced here: 145 us
  starting transfers between devices  75.1 us (51%)
  blocking collectives  32.5 us (22%)
  Pallas kernels  15.8 us (11%)
  waiting for transfers between devices  13.4 us (9%)
  local copies, waits for them, and re-layouts  3.23 us (2%)
  matrix products  2.48 us (2%)
  other arithmetic  1.53 us (1%)
    all_to_all x1, starting transfers between devices, on_device(): got = lax.all_to_all(sent, 'docs', 0, 0, tiled=True)  43.7 us
    all_to_all x1, blocking collectives, docs_exchange(): lax.all_to_all(x, 'docs', 0, 0, axis_index_groups=[members], tiled=True)  20 us
    all_to_all x1, blocking collectives, on_device(): lax.all_to_all(sent, ('mp', 'sub'), 0, 0, axis_index_groups=cells, tiled=...  12.5 us
    all_to_all x1, starting transfers between devices, docs_exchange(): lax.all_to_all(x, 'docs', 0, 0, axis_index_groups=[members], tiled=True)  12 us
    ppermute x2, starting transfers between devices, moved(): return lax.ppermute(x, 'mp', [(i, (i + by) % lanes) for i in range(lanes)])  8.45 us
    all_to_all x1, waiting for transfers between devices, on_device(): got = lax.all_to_all(sent, 'docs', 0, 0, tiled=True)  7.9 us
    all_to_all x1, starting transfers between devices, on_device(): lax.all_to_all(spread, 'mp', 0, 0, axis_index_groups=parities, tiled=True)  6.99 us
    pallas_call x1, Pallas kernels, slopes(): pl.pallas_call(functools.partial(slope_kernel, count), out_shape=(whole((...  4.88 us
  transfers between devices with their start and end apart: 6, of which 3 were waited for; matrix products, arithmetic and copies ran while one was open for 3% of the time, Pallas kernels for 9%

profile of v2, /device:TPU:80, one launch (start us, length us, event | category | flops | bytes accessed | tf_op | source)
XLA Modules:
  0.0 145.0 jit_solution(13719770217405617771)
XLA Ops:
  0.6 4.6 %collective-permute-start = (bf16[128,1024]{1,0:T(8,128)(2,1)}, bf16[128,1024]{1,0:T(8,128)(2,1)S(1)}, u32[]{:S(2)}, u32[]{:S(2)}) collective-permute-start(bf16[128,1024]{1,0:T(8,128)(2,1)} %refs_0_.1), channel_id=1, source_target_pairs={{0,4},{2,6},{4,8},{6,10},{8,12},{10,14},{12,0},{14,2},{1,5},{3,7},... | collective-permute-start | bytes 786440 | tf_op jit(solution)/shard_map/ppermute | solution.py:234
  5.3 3.8 %collective-permute-start.1 = (bf16[128,1024]{1,0:T(8,128)(2,1)}, bf16[128,1024]{1,0:T(8,128)(2,1)S(1)}, u32[]{:S(2)}, u32[]{:S(2)}) collective-permute-start(bf16[128,1024]{1,0:T(8,128)(2,1)} %refs_0_.1), channel_id=1, source_target_pairs={{0,12},{2,14},{4,0},{6,2},{8,4},{10,6},{12,8},{14,10},{1,13},{3,15... | collective-permute-start | bytes 786440 | tf_op jit(solution)/shard_map/ppermute | solution.py:234
  9.1 2.8 %score.1 = (f32[16,8,128]{2,1,0:T(8,128)}, s32[128,1]{1,0:T(8,128)}) custom-call(bf16[128,1024]{1,0:T(8,128)(2,1)} %refs_0_.1, bf16[1024,1024]{1,0:T(8,128)(2,1)} %w1_ref.3, f32[1,1024]{1,0:T(1,128)} %bitcast.28, s32[1,128]{1,0:T(1,128)} %bitcast.30, s32[1,128]{1,0:T(1,128)} %bitcast.31, s32[1,128]{1,0:T(1,128)} %bitcast.32), custom_call_target="tpu_custom_call" | custom-call | tf_op jit(solution)/shard_map/score/pallas_call | solution.py:257
  11.9 43.7 %all-to-all-start = ((f32[16,8,128]{2,1,0:T(8,128)}), f32[16,8,128]{2,1,0:T(8,128)S(1)}, u32[]{:S(2)}, u32[]{:S(2)}) async-start(f32[16,8,128]{2,1,0:T(8,128)} %get-tuple-element.12), calls=%async_computation | async-start | bytes 131072 | tf_op jit(solution)/shard_map/all_to_all | solution.py:270
  55.7 4.0 %collective-permute-start.2 = (bf16[128,1024]{1,0:T(8,128)(2,1)S(1)}, bf16[128,1024]{1,0:T(8,128)(2,1)S(1)}, u32[]{:S(2)}, u32[]{:S(2)}) collective-permute-start(bf16[128,1024]{1,0:T(8,128)(2,1)S(1)} %broadcast_select_fusion), channel_id=1, source_target_pairs={{0,4},{1,13},{2,6},{3,15},{4,8},{5,1},{6,10},{7,3},{8,12},{9,5},{1... | collective-permute-start | bytes 786440 | tf_op jit(solution)/shard_map/ppermute | solution.py:243
  59.7 0.6 pad_add_fusion.place_ref
  60.2 7.9 %all-to-all-done.got_ref = f32[16,8,128]{2,1,0:T(8,128)S(1)} async-done(((f32[16,8,128]{2,1,0:T(8,128)}), f32[16,8,128]{2,1,0:T(8,128)S(1)}, u32[]{:S(2)}, u32[]{:S(2)}) %all-to-all-start) | async-done | bytes 65568 | tf_op jit(solution)/shard_map/all_to_all | solution.py:270
  68.1 0.6 copy-done.3
  68.7 4.7 %lambdas.1 = (f32[4,8,128]{2,1,0:T(8,128)}, f32[128,1]{1,0:T(8,128)}) custom-call(s32[3]{0:T(128)} %pad_add_fusion.place_ref, f32[16,8,128]{2,1,0:T(8,128)} %copy-done.3, s32[128,1]{1,0:T(8,128)} %get-tuple-element.13.slot_ref), custom_call_target="tpu_custom_call" | custom-call | tf_op jit(solution)/shard_map/lambdas/pallas_call | solution.py:271
  73.4 7.0 %all-to-all-start.1 = ((f32[4,8,128]{2,1,0:T(8,128)}), f32[4,8,128]{2,1,0:T(8,128)S(1)}, u32[]{:S(2)}, u32[]{:S(2)}) async-start(f32[4,8,128]{2,1,0:T(8,128)} %get-tuple-element.15), calls=%async_computation.1 | async-start | bytes 32768 | tf_op jit(solution)/shard_map/all_to_all | solution.py:281
  80.5 0.7 copy-done.4
  81.2 4.9 %slopes.1 = (bf16[4,128,1024]{2,1,0:T(8,128)(2,1)}, bf16[4,128,1024]{2,1,0:T(8,128)(2,1)}, bf16[4,128,256]{2,1,0:T(8,128)(2,1)}) custom-call(s32[3]{0:T(128)} %pad_add_fusion.place_ref, bf16[1024,1024]{1,0:T(8,128)(2,1)} %w1_ref.3, f32[1,1024]{1,0:T(1,128)} %bitcast.29, bf16[128,1024]{1,0:T(8,128)(2,1)} %refs_0_.1, bf16[128,1024]{1,0:T(8,128)(2,1)} %copy-done.1, ...), custom_call_target="tpu_custom_call" | custom-call | tf_op jit(solution)/shard_map/slopes/pallas_call | solution.py:173
  86.0 2.2 %all-to-all-done.1.lambda_ref = f32[4,8,128]{2,1,0:T(8,128)S(1)} async-done(((f32[4,8,128]{2,1,0:T(8,128)}), f32[4,8,128]{2,1,0:T(8,128)S(1)}, u32[]{:S(2)}, u32[]{:S(2)}) %all-to-all-start.1) | async-done | bytes 16416 | tf_op jit(solution)/shard_map/all_to_all | solution.py:281
  88.2 0.6 copy-done.5
  88.8 3.5 %product.1 = bf16[4,520,128]{2,1,0:T(8,128)(2,1)} custom-call(s32[3]{0:T(128)} %pad_add_fusion.place_ref, f32[4,8,128]{2,1,0:T(8,128)} %copy-done.5, bf16[4,128,1024]{2,1,0:T(8,128)(2,1)} %get-tuple-element.16.refs_0_, bf16[4,128,1024]{2,1,0:T(8,128)(2,1)} %get-tuple-element.17.refs_1_, bf16[4,128,256]{2,1,0:T(8,128)(2,1)} %get-tuple-element.18.refs_2_), custom_call_target="tpu_custom_call" | custom-call | tf_op jit(solution)/shard_map/product/pallas_call | solution.py:291
  92.3 12.5 %all_to_all.25 = bf16[4,520,128]{2,1,0:T(8,128)(2,1)S(1)} all-to-all(bf16[4,520,128]{2,1,0:T(8,128)(2,1)} %product.1), channel_id=1, replica_groups={{0,1,2,3},{4,5,6,7},{8,9,10,11},{12,13,14,15},{16,17,18,19},{20,21,22,2..., dimensions={0} | all-to-all | bytes 1064960 | tf_op jit(solution)/shard_map/all_to_all | solution.py:299
  104.9 20.0 %all_to_all.26 = bf16[16,40,128]{2,1,0:T(8,128)(2,1)S(1)} all-to-all(bf16[16,40,128]{2,1,0:T(8,128)(2,1)S(1)} %pad_maximum_fusion), channel_id=1, replica_groups={{128,144,160,176,192,208,224,240,0,16,32,48,64,80,96,112},{129,145,161,..., dimensions={0} | all-to-all | bytes 327680 | tf_op jit(solution)/shard_map/all_to_all | solution.py:227
  125.0 0.7 broadcast_in_dim.5
  125.6 12.0 %all-to-all-start.4 = ((bf16[16,32,128]{2,1,0:T(8,128)(2,1)}), bf16[16,32,128]{2,1,0:T(8,128)(2,1)S(1)}, u32[]{:S(2)}, u32[]{:S(2)}) async-start(bf16[16,32,128]{2,1,0:T(8,128)(2,1)} %broadcast_in_dim.5), calls=%async_computation.4 | async-start | bytes 262144 | tf_op jit(solution)/shard_map/all_to_all | solution.py:227
  137.7 0.1 reduce.1
  137.8 0.6 slice_bitcast_fusion
  138.4 2.5 %fusion = bf16[128,1024]{1,0:T(8,128)(2,1)} fusion(bf16[1024,1024]{1,0:T(8,128)(2,1)S(1)} %copy-done, bf16[4,128,1024]{2,1,0:T(8,128)(2,1)} %get-tuple-element.16.refs_0_, f32[128]{0:T(128)S(1)} %reduce.1), kind=kOutput, calls=%fused_computation.1 | convolution fusion | flops 268697600 | bytes 2621952 | tf_op jit(solution)/shard_map/dot_general | solution.py:309
  140.9 3.4 %all-to-all-done.4 = bf16[16,32,128]{2,1,0:T(8,128)(2,1)S(1)} async-done(((bf16[16,32,128]{2,1,0:T(8,128)(2,1)}), bf16[16,32,128]{2,1,0:T(8,128)(2,1)S(1)}, u32[]{:S(2)}, u32[]{:S(2)}) %all-to-all-start.4) | async-done | bytes 131104 | tf_op jit(solution)/shard_map/all_to_all | solution.py:227
  144.3 0.7 copy_bitcast_fusion
  (22 shorter events, 0.2 us)
Async XLA Ops:
  0.6 55.0 %collective-permute-start = (bf16[128,1024]{1,0:T(8,128)(2,1)}, bf16[128,1024]{1,0:T(8,128)(2,1)S(1)}, u32[]{:S(2)}, u32[]{:S(2)}) collective-permute-start(bf16[128,1024]{1,0:T(8,128)(2,1)} %refs_0_.1), channel_id=1, source_target_pairs={{0,4},{2,6},{4,8},{6,10},{8,12},{10,14},{12,0},{14,2},{1,5},{3,7},... | collective-permute-start | bytes 786440 | tf_op jit(solution)/shard_map/ppermute | solution.py:234
  5.3 50.3 %collective-permute-start.1 = (bf16[128,1024]{1,0:T(8,128)(2,1)}, bf16[128,1024]{1,0:T(8,128)(2,1)S(1)}, u32[]{:S(2)}, u32[]{:S(2)}) collective-permute-start(bf16[128,1024]{1,0:T(8,128)(2,1)} %refs_0_.1), channel_id=1, source_target_pairs={{0,12},{2,14},{4,0},{6,2},{8,4},{10,6},{12,8},{14,10},{1,13},{3,15... | collective-permute-start | bytes 786440 | tf_op jit(solution)/shard_map/ppermute | solution.py:234
  11.9 56.2 %all-to-all-start = ((f32[16,8,128]{2,1,0:T(8,128)}), f32[16,8,128]{2,1,0:T(8,128)S(1)}, u32[]{:S(2)}, u32[]{:S(2)}) async-start(f32[16,8,128]{2,1,0:T(8,128)} %get-tuple-element.12), calls=%async_computation | async-start | bytes 131072 | tf_op jit(solution)/shard_map/all_to_all | solution.py:270
  55.6 24.8 %copy-start.1 = (bf16[128,1024]{1,0:T(8,128)(2,1)}, bf16[128,1024]{1,0:T(8,128)(2,1)S(1)}, u32[]{:S(2)}) copy-start(bf16[128,1024]{1,0:T(8,128)(2,1)S(1)} %collective-permute-done.refs_1_) | copy-start | bytes 786436
  55.6 24.8 %copy-start.2 = (bf16[128,1024]{1,0:T(8,128)(2,1)}, bf16[128,1024]{1,0:T(8,128)(2,1)S(1)}, u32[]{:S(2)}) copy-start(bf16[128,1024]{1,0:T(8,128)(2,1)S(1)} %collective-permute-done.1.refs_2_) | copy-start | bytes 786436
  55.7 24.8 %collective-permute-start.2 = (bf16[128,1024]{1,0:T(8,128)(2,1)S(1)}, bf16[128,1024]{1,0:T(8,128)(2,1)S(1)}, u32[]{:S(2)}, u32[]{:S(2)}) collective-permute-start(bf16[128,1024]{1,0:T(8,128)(2,1)S(1)} %broadcast_select_fusion), channel_id=1, source_target_pairs={{0,4},{1,13},{2,6},{3,15},{4,8},{5,1},{6,10},{7,3},{8,12},{9,5},{1... | collective-permute-start | bytes 786440 | tf_op jit(solution)/shard_map/ppermute | solution.py:243
  68.1 0.6 copy-start.3
  73.4 14.8 %all-to-all-start.1 = ((f32[4,8,128]{2,1,0:T(8,128)}), f32[4,8,128]{2,1,0:T(8,128)S(1)}, u32[]{:S(2)}, u32[]{:S(2)}) async-start(f32[4,8,128]{2,1,0:T(8,128)} %get-tuple-element.15), calls=%async_computation.1 | async-start | bytes 32768 | tf_op jit(solution)/shard_map/all_to_all | solution.py:281
  80.5 0.7 copy-start.4
  88.2 0.6 copy-start.5
  92.3 45.4 %copy-start.6 = (f32[128,1]{1,0:T(8,128)S(1)}, f32[128,1]{1,0:T(8,128)}, u32[]{:S(2)}) copy-start(f32[128,1]{1,0:T(8,128)} %get-tuple-element.19) | copy-start | bytes 1540
  92.3 46.1 %copy-start = (bf16[1024,1024]{1,0:T(8,128)(2,1)S(1)}, bf16[1024,1024]{1,0:T(8,128)(2,1)}, u32[]{:S(2)}) copy-start(bf16[1024,1024]{1,0:T(8,128)(2,1)} %w1_ref.3) | copy-start | bytes 6291460
  125.6 18.6 %all-to-all-start.4 = ((bf16[16,32,128]{2,1,0:T(8,128)(2,1)}), bf16[16,32,128]{2,1,0:T(8,128)(2,1)S(1)}, u32[]{:S(2)}, u32[]{:S(2)}) async-start(bf16[16,32,128]{2,1,0:T(8,128)(2,1)} %broadcast_in_dim.5), calls=%async_computation.4 | async-start | bytes 262144 | tf_op jit(solution)/shard_map/all_to_all | solution.py:227

commit v3 on v1

--- a/solution.py
+++ b/solution.py
@@ -15,39 +15,55 @@
     return jax.ShapeDtypeStruct(*shape_and_type)
 
 
+def on_chip(x):
+    return pltpu.with_memory_space_constraint(x, pltpu.VMEM)
+
+
 def vmem_specs(count):
     return [pl.BlockSpec(memory_space=pltpu.VMEM)] * count
 
 
-def score_kernel(capacity, emb_ref, w1_ref, w2_ref, owner_ref, query_ref, label_ref, sent_ref, slot_ref):
+def score_kernel(
+    capacity, emb_ref, w1_ref, w2_ref, owner_ref, query_ref, label_ref, sent_ref, slot_ref, sum_ref
+):
     rows = emb_ref.shape[0]
-    halves = sent_ref.shape[1] // 4
-    along = lax.broadcasted_iota(jnp.int32, (rows, rows), 1)
-    down = lax.broadcasted_iota(jnp.int32, (rows, rows), 0)
-
-    def column(row):
-        return jnp.sum(jnp.where(along == down, row, 0), axis=1, keepdims=True)
-
-    owner = owner_ref[...]
-    owner_column = column(owner)
-    earlier = jnp.where((owner_column == owner) & (along < down), 1, 0)
-    slot = owner_column * capacity + jnp.sum(earlier, axis=1, keepdims=True)
-    slot_ref[...] = slot
-    mark = column(query_ref[...] + 1).astype(jnp.float32)
-    label = column(label_ref[...]).astype(jnp.float32)
+    targets, halves = sent_ref.shape[0], sent_ref.shape[1] // 4
+    lane = lax.broadcasted_iota(jnp.int32, (rows, LANES), 1)
+
+    def send(place, value):
+        for h in range(halves):
+            here = slot_ref[...] == lane + h * LANES
+            row = jnp.sum(jnp.where(here, value, 0.0), axis=0, keepdims=True)
+            for target in range(targets):
+                sent_ref[target, place * halves + h : place * halves + h + 1, :] = row
+
+    @pl.when(pl.program_id(0) == 0)
+    def _():
+        along = lax.broadcasted_iota(jnp.int32, (rows, rows), 1)
+        down = lax.broadcasted_iota(jnp.int32, (rows, rows), 0)
+
+        def column(row):
+            return jnp.sum(jnp.where(along == down, row, 0), axis=1, keepdims=True)
+
+        owner = owner_ref[...]
+        owner_column = column(owner)
+        earlier = jnp.where((owner_column == owner) & (along < down), 1, 0)
+        slot_ref[...] = owner_column * capacity + jnp.sum(earlier, axis=1, keepdims=True)
+        sum_ref[...] = jnp.zeros_like(sum_ref)
+        sent_ref[...] = jnp.zeros_like(sent_ref)
+        send(1, column(query_ref[...] + 1).astype(jnp.float32))
+        send(2, column(label_ref[...]).astype(jnp.float32))
 
     pre_act = jnp.dot(emb_ref[...], w1_ref[...], preferred_element_type=jnp.float32)
-    hidden = pre_act * jax.nn.sigmoid(pre_act)
-    score = jnp.sum(hidden * w2_ref[...], axis=1, keepdims=True)
-
-    lane = lax.broadcasted_iota(jnp.int32, (rows, LANES), 1)
-    sent_ref[...] = jnp.zeros_like(sent_ref)
-    for h in range(halves):
-        here = slot == lane + h * LANES
-        for place, value in enumerate((score, mark, label)):
-            row = jnp.sum(jnp.where(here, value, 0.0), axis=0, keepdims=True)
-            for target in range(sent_ref.shape[0]):
-                sent_ref[target, place * halves + h : place * halves + h + 1, :] = row
+    weighted = pre_act * jax.nn.sigmoid(pre_act) * w2_ref[...]
+    part = sum_ref[...]
+    for k in range(weighted.shape[1] // LANES):
+        part = part + weighted[:, k * LANES : (k + 1) * LANES]
+    sum_ref[...] = part
+
+    @pl.when(pl.program_id(0) == pl.num_programs(0) - 1)
+    def _():
+        send(0, jnp.sum(sum_ref[...], axis=1, keepdims=True))
 
 
 def within_groups(x, capacity):
@@ -253,14 +269,28 @@
     place = jnp.stack([lax.axis_index(axis) for axis in ("docs", "mp", "sub")]).astype(jnp.int32)
     back, on, across = parity_blocks(embeddings)
     members = lanes // 2
+    steps = 4
+
+    def fixed(*shape):
+        return pl.BlockSpec(shape, lambda j: (0,) * len(shape))
+
     sent, slot = pl.pallas_call(
         functools.partial(score_kernel, capacity),
+        grid=(steps,),
         out_shape=(
             whole((docs, 4 * halves, LANES), jnp.float32),
             whole((rows, 1), jnp.int32),
         ),
-        in_specs=vmem_specs(6),
-        out_specs=tuple(vmem_specs(2)),
+        in_specs=[
+            fixed(rows, width),
+            pl.BlockSpec((width, units // steps), lambda j: (0, j)),
+            pl.BlockSpec((1, units // steps), lambda j: (0, j)),
+            fixed(1, rows),
+            fixed(1, rows),
+            fixed(1, rows),
+        ],
+        out_specs=(fixed(docs, 4 * halves, LANES), fixed(rows, 1)),
+        scratch_shapes=[pltpu.VMEM((rows, LANES), jnp.float32)],
         name="score",
     )(
         embeddings, w_first, w2_row,
@@ -275,7 +305,7 @@
         scratch_shapes=[pltpu.VMEM((docs * capacity, LANES), jnp.float32)] * 4
         + [pltpu.VMEM((4 * docs, LANES), jnp.float32)],
         name="lambdas",
-    )(place, got, slot)
+    )(place, on_chip(got), slot)
     parities = [list(range(parity, lanes, 2)) for parity in range(2)]
     all_lambdas = lax.all_to_all(
         spread, "mp", 0, 0, axis_index_groups=parities, tiled=True
@@ -289,11 +319,11 @@
     offsets = ((0, members - 1, 1, 2),)
     sent = pl.pallas_call(
         functools.partial(product_kernel, offsets),
-        out_shape=whole((targets, (part_rows + 1) * columns, LANES), jnp.bfloat16),
+        out_shape=pltpu.VMEM((targets, (part_rows + 1) * columns, LANES), jnp.bfloat16),
         in_specs=[pl.BlockSpec(memory_space=pltpu.SMEM)] + vmem_specs(4),
         out_specs=vmem_specs(1)[0],
         name="product",
-    )(place, all_lambdas, *prepared)
+    )(place, on_chip(all_lambdas), *prepared)
     cells = [list(range(i, i + targets)) for i in range(0, lanes * subs, targets)]
     arrived = lax.all_to_all(
         sent, ("mp", "sub"), 0, 0, axis_index_groups=cells, tiled=True

time: 145 us -> 143 us (0.986)
  transfers between devices with their start and end apart: 6 -> 6, of which waited for: 3 -> 3; matrix products, arithmetic and copies ran while one was open for 3% -> 3% of each run, Pallas kernels for 9% -> 10%
where the time goes in v3:
time: 143 us
  starting transfers between devices  68.6 us (48%)
  blocking collectives  29.4 us (21%)
  waiting for transfers between devices  21.5 us (15%)
  Pallas kernels  16.5 us (12%)
  matrix products  2.48 us (2%)
  local copies, waits for them, and re-layouts  2.02 us (1%)
  other arithmetic  1.53 us (1%)
    all_to_all x1, starting transfers between devices, on_device(): got = lax.all_to_all(sent, 'docs', 0, 0, tiled=True)  43.7 us
    all_to_all x1, blocking collectives, on_device(): lax.all_to_all(jnp.concatenate([tiles, second], axis=1), 'docs', 0, 0, ti...  17.9 us
    all_to_all x1, blocking collectives, on_device(): lax.all_to_all(sent, ('mp', 'sub'), 0, 0, axis_index_groups=cells, tiled=...  11.5 us
    all_to_all x1, waiting for transfers between devices, sent_to_all(): lax.all_to_all(jnp.broadcast_to(x[None], (count, *x.shape)), axis, 0, 0,...  11.4 us
    ppermute x2, starting transfers between devices, moved(): return lax.ppermute(x, 'mp', [(i, (i + by) % lanes) for i in range(lanes)])  8.45 us
    all_to_all x1, waiting for transfers between devices, on_device(): got = lax.all_to_all(sent, 'docs', 0, 0, tiled=True)  7.9 us
    all_to_all x1, starting transfers between devices, on_device(): lax.all_to_all(spread, 'mp', 0, 0, axis_index_groups=parities, tiled=True)  6.99 us
    all_to_all x1, starting transfers between devices, sent_to_all(): lax.all_to_all(jnp.broadcast_to(x[None], (count, *x.shape)), axis, 0, 0,...  5.45 us
  transfers between devices with their start and end apart: 6, of which 3 were waited for; matrix products, arithmetic and copies ran while one was open for 3% of the time, Pallas kernels for 10%

profile of v3, /device:TPU:80, one launch (start us, length us, event | category | flops | bytes accessed | tf_op | source)
XLA Modules:
  0.0 142.7 jit_solution(16935834580129621021)
XLA Ops:
  0.6 4.6 %collective-permute-start = (bf16[128,1024]{1,0:T(8,128)(2,1)}, bf16[128,1024]{1,0:T(8,128)(2,1)S(1)}, u32[]{:S(2)}, u32[]{:S(2)}) collective-permute-start(bf16[128,1024]{1,0:T(8,128)(2,1)} %refs_0_.1), channel_id=1, source_target_pairs={{0,4},{2,6},{4,8},{6,10},{8,12},{10,14},{12,0},{14,2},{1,5},{3,7},... | collective-permute-start | bytes 786440 | tf_op jit(solution)/shard_map/ppermute | solution.py:249
  5.3 3.8 %collective-permute-start.1 = (bf16[128,1024]{1,0:T(8,128)(2,1)}, bf16[128,1024]{1,0:T(8,128)(2,1)S(1)}, u32[]{:S(2)}, u32[]{:S(2)}) collective-permute-start(bf16[128,1024]{1,0:T(8,128)(2,1)} %refs_0_.1), channel_id=1, source_target_pairs={{0,12},{2,14},{4,0},{6,2},{8,4},{10,6},{12,8},{14,10},{1,13},{3,15... | collective-permute-start | bytes 786440 | tf_op jit(solution)/shard_map/ppermute | solution.py:249
  9.1 4.3 %score.1 = (f32[16,8,128]{2,1,0:T(8,128)}, s32[128,1]{1,0:T(8,128)}) custom-call(bf16[128,1024]{1,0:T(8,128)(2,1)} %refs_0_.1, bf16[1024,1024]{1,0:T(8,128)(2,1)} %w1_ref.3, f32[1,1024]{1,0:T(1,128)} %bitcast.28, s32[1,128]{1,0:T(1,128)} %bitcast.30, s32[1,128]{1,0:T(1,128)} %bitcast.31, s32[1,128]{1,0:T(1,128)} %bitcast.32), custom_call_target="tpu_custom_call" | custom-call | tf_op jit(solution)/shard_map/score/pallas_call | solution.py:277
  13.4 43.7 %all-to-all-start = ((f32[16,8,128]{2,1,0:T(8,128)}), f32[16,8,128]{2,1,0:T(8,128)S(1)}, u32[]{:S(2)}, u32[]{:S(2)}) async-start(f32[16,8,128]{2,1,0:T(8,128)} %get-tuple-element.12), calls=%async_computation | async-start | bytes 131072 | tf_op jit(solution)/shard_map/all_to_all | solution.py:299
  57.1 0.0 copy-start.2
  57.1 4.0 %collective-permute-start.2 = (bf16[128,1024]{1,0:T(8,128)(2,1)S(1)}, bf16[128,1024]{1,0:T(8,128)(2,1)S(1)}, u32[]{:S(2)}, u32[]{:S(2)}) collective-permute-start(bf16[128,1024]{1,0:T(8,128)(2,1)S(1)} %broadcast_select_fusion), channel_id=1, source_target_pairs={{0,4},{1,13},{2,6},{3,15},{4,8},{5,1},{6,10},{7,3},{8,12},{9,5},{1... | collective-permute-start | bytes 786440 | tf_op jit(solution)/shard_map/ppermute | solution.py:258
  61.1 0.6 pad_add_fusion.place_ref
  61.7 7.9 %all-to-all-done.got_ref = f32[16,8,128]{2,1,0:T(8,128)S(1)} async-done(((f32[16,8,128]{2,1,0:T(8,128)}), f32[16,8,128]{2,1,0:T(8,128)S(1)}, u32[]{:S(2)}, u32[]{:S(2)}) %all-to-all-start) | async-done | bytes 65568 | tf_op jit(solution)/shard_map/all_to_all | solution.py:299
  69.6 4.7 %lambdas.1 = (f32[4,8,128]{2,1,0:T(8,128)}, f32[128,1]{1,0:T(8,128)}) custom-call(s32[3]{0:T(128)} %pad_add_fusion.place_ref, f32[16,8,128]{2,1,0:T(8,128)S(1)} %all-to-all-done.got_ref, s32[128,1]{1,0:T(8,128)} %get-tuple-element.13.slot_ref), custom_call_target="tpu_custom_call" | custom-call | tf_op jit(solution)/shard_map/lambdas/pallas_call | solution.py:300
  74.3 7.0 %all-to-all-start.1 = ((f32[4,8,128]{2,1,0:T(8,128)}), f32[4,8,128]{2,1,0:T(8,128)S(1)}, u32[]{:S(2)}, u32[]{:S(2)}) async-start(f32[4,8,128]{2,1,0:T(8,128)} %get-tuple-element.15), calls=%async_computation.1 | async-start | bytes 32768 | tf_op jit(solution)/shard_map/all_to_all | solution.py:310
  81.3 0.7 copy-done.3
  82.0 4.9 %slopes.1 = (bf16[4,128,1024]{2,1,0:T(8,128)(2,1)}, bf16[4,128,1024]{2,1,0:T(8,128)(2,1)}, bf16[4,128,256]{2,1,0:T(8,128)(2,1)}) custom-call(s32[3]{0:T(128)} %pad_add_fusion.place_ref, bf16[1024,1024]{1,0:T(8,128)(2,1)} %w1_ref.3, f32[1,1024]{1,0:T(1,128)} %bitcast.29, bf16[128,1024]{1,0:T(8,128)(2,1)} %refs_0_.1, bf16[128,1024]{1,0:T(8,128)(2,1)} %copy-done.1, ...), custom_call_target="tpu_custom_call" | custom-call | tf_op jit(solution)/shard_map/slopes/pallas_call | solution.py:189
  86.9 2.1 %all-to-all-done.1.lambda_ref = f32[4,8,128]{2,1,0:T(8,128)S(1)} async-done(((f32[4,8,128]{2,1,0:T(8,128)}), f32[4,8,128]{2,1,0:T(8,128)S(1)}, u32[]{:S(2)}, u32[]{:S(2)}) %all-to-all-start.1) | async-done | bytes 16416 | tf_op jit(solution)/shard_map/all_to_all | solution.py:310
  89.0 2.6 %product.1 = bf16[4,520,128]{2,1,0:T(8,128)(2,1)S(1)} custom-call(s32[3]{0:T(128)} %pad_add_fusion.place_ref, f32[4,8,128]{2,1,0:T(8,128)S(1)} %all-to-all-done.1.lambda_ref, bf16[4,128,1024]{2,1,0:T(8,128)(2,1)} %get-tuple-element.16.refs_0_, bf16[4,128,1024]{2,1,0:T(8,128)(2,1)} %get-tuple-element.17.refs_1_, bf16[4,128,256]{2,1,0:T(8,128)(2,1)} %get-tuple-element.18.refs_2_), custom_call_target="tpu_custom_call" | custom-call | tf_op jit(solution)/shard_map/product/pallas_call | solution.py:320
  91.7 11.5 %all_to_all.25 = bf16[4,520,128]{2,1,0:T(8,128)(2,1)S(1)} all-to-all(bf16[4,520,128]{2,1,0:T(8,128)(2,1)S(1)} %product.1), channel_id=1, replica_groups={{0,1,2,3},{4,5,6,7},{8,9,10,11},{12,13,14,15},{16,17,18,19},{20,21,22,2..., dimensions={0} | all-to-all | bytes 1064960 | tf_op jit(solution)/shard_map/all_to_all | solution.py:328
  103.2 0.1 reduce_sum.21
  103.3 17.9 %all_to_all.26 = bf16[16,40,128]{2,1,0:T(8,128)(2,1)S(1)} all-to-all(bf16[16,40,128]{2,1,0:T(8,128)(2,1)S(1)} %pad_maximum_fusion), channel_id=1, replica_groups=mesh['groups'=2,'docs'=16,'mp'=8,'sub'=2] {'docs'}, dimensions={0} | all-to-all | bytes 327680 | tf_op jit(solution)/shard_map/all_to_all | solution.py:335
  121.3 0.7 broadcast_in_dim.5
  121.9 5.5 %all-to-all-start.4 = ((bf16[16,32,128]{2,1,0:T(8,128)(2,1)}), bf16[16,32,128]{2,1,0:T(8,128)(2,1)S(1)}, u32[]{:S(2)}, u32[]{:S(2)}) async-start(bf16[16,32,128]{2,1,0:T(8,128)(2,1)} %broadcast_in_dim.5), calls=%async_computation.4 | async-start | bytes 262144 | tf_op jit(solution)/shard_map/all_to_all | solution.py:242
  127.4 0.1 reduce.1
  127.5 0.6 slice_bitcast_fusion
  128.1 2.5 %fusion = bf16[128,1024]{1,0:T(8,128)(2,1)} fusion(bf16[1024,1024]{1,0:T(8,128)(2,1)S(1)} %copy-done, bf16[4,128,1024]{2,1,0:T(8,128)(2,1)} %get-tuple-element.16.refs_0_, f32[128]{0:T(128)S(1)} %reduce.1), kind=kOutput, calls=%fused_computation.1 | convolution fusion | flops 268697600 | bytes 2621952 | tf_op jit(solution)/shard_map/dot_general | solution.py:338
  130.6 11.4 %all-to-all-done.4 = bf16[16,32,128]{2,1,0:T(8,128)(2,1)S(1)} async-done(((bf16[16,32,128]{2,1,0:T(8,128)(2,1)}), bf16[16,32,128]{2,1,0:T(8,128)(2,1)S(1)}, u32[]{:S(2)}, u32[]{:S(2)}) %all-to-all-start.4) | async-done | bytes 131104 | tf_op jit(solution)/shard_map/all_to_all | solution.py:242
  142.0 0.7 copy_bitcast_fusion
  (18 shorter events, 0.1 us)
Async XLA Ops:
  0.6 56.4 %collective-permute-start = (bf16[128,1024]{1,0:T(8,128)(2,1)}, bf16[128,1024]{1,0:T(8,128)(2,1)S(1)}, u32[]{:S(2)}, u32[]{:S(2)}) collective-permute-start(bf16[128,1024]{1,0:T(8,128)(2,1)} %refs_0_.1), channel_id=1, source_target_pairs={{0,4},{2,6},{4,8},{6,10},{8,12},{10,14},{12,0},{14,2},{1,5},{3,7},... | collective-permute-start | bytes 786440 | tf_op jit(solution)/shard_map/ppermute | solution.py:249
  5.3 51.8 %collective-permute-start.1 = (bf16[128,1024]{1,0:T(8,128)(2,1)}, bf16[128,1024]{1,0:T(8,128)(2,1)S(1)}, u32[]{:S(2)}, u32[]{:S(2)}) collective-permute-start(bf16[128,1024]{1,0:T(8,128)(2,1)} %refs_0_.1), channel_id=1, source_target_pairs={{0,12},{2,14},{4,0},{6,2},{8,4},{10,6},{12,8},{14,10},{1,13},{3,15... | collective-permute-start | bytes 786440 | tf_op jit(solution)/shard_map/ppermute | solution.py:249
  13.4 56.2 %all-to-all-start = ((f32[16,8,128]{2,1,0:T(8,128)}), f32[16,8,128]{2,1,0:T(8,128)S(1)}, u32[]{:S(2)}, u32[]{:S(2)}) async-start(f32[16,8,128]{2,1,0:T(8,128)} %get-tuple-element.12), calls=%async_computation | async-start | bytes 131072 | tf_op jit(solution)/shard_map/all_to_all | solution.py:299
  57.1 24.2 %copy-start.1 = (bf16[128,1024]{1,0:T(8,128)(2,1)}, bf16[128,1024]{1,0:T(8,128)(2,1)S(1)}, u32[]{:S(2)}) copy-start(bf16[128,1024]{1,0:T(8,128)(2,1)S(1)} %collective-permute-done.refs_1_) | copy-start | bytes 786436
  57.1 24.2 %copy-start.2 = (bf16[128,1024]{1,0:T(8,128)(2,1)}, bf16[128,1024]{1,0:T(8,128)(2,1)S(1)}, u32[]{:S(2)}) copy-start(bf16[128,1024]{1,0:T(8,128)(2,1)S(1)} %collective-permute-done.1.refs_2_) | copy-start | bytes 786436
  57.1 24.1 %collective-permute-start.2 = (bf16[128,1024]{1,0:T(8,128)(2,1)S(1)}, bf16[128,1024]{1,0:T(8,128)(2,1)S(1)}, u32[]{:S(2)}, u32[]{:S(2)}) collective-permute-start(bf16[128,1024]{1,0:T(8,128)(2,1)S(1)} %broadcast_select_fusion), channel_id=1, source_target_pairs={{0,4},{1,13},{2,6},{3,15},{4,8},{5,1},{6,10},{7,3},{8,12},{9,5},{1... | collective-permute-start | bytes 786440 | tf_op jit(solution)/shard_map/ppermute | solution.py:258
  74.3 14.8 %all-to-all-start.1 = ((f32[4,8,128]{2,1,0:T(8,128)}), f32[4,8,128]{2,1,0:T(8,128)S(1)}, u32[]{:S(2)}, u32[]{:S(2)}) async-start(f32[4,8,128]{2,1,0:T(8,128)} %get-tuple-element.15), calls=%async_computation.1 | async-start | bytes 32768 | tf_op jit(solution)/shard_map/all_to_all | solution.py:310
  81.3 0.7 copy-start.3
  91.7 35.7 %copy-start.4 = (f32[128,1]{1,0:T(8,128)S(1)}, f32[128,1]{1,0:T(8,128)}, u32[]{:S(2)}) copy-start(f32[128,1]{1,0:T(8,128)} %get-tuple-element.19) | copy-start | bytes 1540
  91.7 36.4 %copy-start = (bf16[1024,1024]{1,0:T(8,128)(2,1)S(1)}, bf16[1024,1024]{1,0:T(8,128)(2,1)}, u32[]{:S(2)}) copy-start(bf16[1024,1024]{1,0:T(8,128)(2,1)} %w1_ref.3) | copy-start | bytes 6291460
  121.9 20.1 %all-to-all-start.4 = ((bf16[16,32,128]{2,1,0:T(8,128)(2,1)}), bf16[16,32,128]{2,1,0:T(8,128)(2,1)S(1)}, u32[]{:S(2)}, u32[]{:S(2)}) async-start(bf16[16,32,128]{2,1,0:T(8,128)(2,1)} %broadcast_in_dim.5), calls=%async_computation.4 | async-start | bytes 262144 | tf_op jit(solution)/shard_map/all_to_all | solution.py:242

commit v4 on v1

--- a/solution.py
+++ b/solution.py
@@ -13,6 +13,10 @@
 
 def whole(*shape_and_type):
     return jax.ShapeDtypeStruct(*shape_and_type)
+
+
+def on_chip(x):
+    return pltpu.with_memory_space_constraint(x, pltpu.VMEM)
 
 
 def vmem_specs(count):
@@ -151,7 +155,7 @@
     along = lax.broadcasted_iota(jnp.int32, (rows, rows), 1)
     down = lax.broadcasted_iota(jnp.int32, (rows, rows), 0)
     row = jnp.sum(jnp.where(along == down, lambda_column, 0.0), axis=0, keepdims=True)
-    spread_ref[...] = jnp.broadcast_to(row[None], spread_ref.shape)
+    spread_ref[...] = jnp.broadcast_to(row, spread_ref.shape)
 
 
 def slope_kernel(count, place_ref, w1_ref, w2_ref, *refs):
@@ -183,30 +187,27 @@
     )(place, w_first, w2_row, *blocks)
 
 
-def product_kernel(groups, place_ref, lambda_ref, *refs):
-    inputs, sent_ref = refs[: 3 * len(groups)], refs[-1]
-    members, rows = lambda_ref.shape[0], lambda_ref.shape[2]
-    my_member = place_ref[1] // 2
+def product_kernel(*refs):
+    lambda_refs, (slope_ref, hidden_ref, part_ref, sent_ref) = refs[:-4], refs[-4:]
+    rows = part_ref.shape[1]
     along = lax.broadcasted_iota(jnp.int32, (rows, rows), 1)
     down = lax.broadcasted_iota(jnp.int32, (rows, rows), 0)
     total, second = None, None
-    for g, offsets in enumerate(groups):
-        slope_ref, hidden_ref, part_ref = inputs[3 * g : 3 * g + 3]
-        for i, offset in enumerate(offsets):
-            block = lambda_ref[lax.rem(my_member + offset, members)]
-            column = jnp.sum(jnp.where(along == down, block[:1], 0.0), axis=1, keepdims=True)
-            part = (part_ref[i].astype(jnp.float32) * column).astype(jnp.bfloat16)
-            product = lax.dot_general(
-                part, slope_ref[i], (((0,), (0,)), ((), ())), preferred_element_type=jnp.float32
-            )
-            high = block.astype(jnp.bfloat16)
-            low = (block - high.astype(jnp.float32)).astype(jnp.bfloat16)
-            hidden = hidden_ref[i]
-            summed = jnp.dot(high, hidden, preferred_element_type=jnp.float32) + jnp.dot(
-                low, hidden, preferred_element_type=jnp.float32
-            )
-            total = product if total is None else total + product
-            second = summed if second is None else second + summed
+    for i, lambda_ref in enumerate(lambda_refs):
+        block = lambda_ref[...]
+        column = jnp.sum(jnp.where(along == down, block[:1], 0.0), axis=1, keepdims=True)
+        part = (part_ref[i].astype(jnp.float32) * column).astype(jnp.bfloat16)
+        product = lax.dot_general(
+            part, slope_ref[i], (((0,), (0,)), ((), ())), preferred_element_type=jnp.float32
+        )
+        high = block.astype(jnp.bfloat16)
+        low = (block - high.astype(jnp.float32)).astype(jnp.bfloat16)
+        hidden = hidden_ref[i]
+        summed = jnp.dot(high, hidden, preferred_element_type=jnp.float32) + jnp.dot(
+            low, hidden, preferred_element_type=jnp.float32
+        )
+        total = product if total is None else total + product
+        second = summed if second is None else second + summed
     targets = sent_ref.shape[0]
     part_rows = total.shape[0] // targets
     columns = total.shape[1] // LANES
@@ -252,7 +253,6 @@
     w2_row = w_second.reshape(1, units)
     place = jnp.stack([lax.axis_index(axis) for axis in ("docs", "mp", "sub")]).astype(jnp.int32)
     back, on, across = parity_blocks(embeddings)
-    members = lanes // 2
     sent, slot = pl.pallas_call(
         functools.partial(score_kernel, capacity),
         out_shape=(
@@ -269,31 +269,31 @@
     got = lax.all_to_all(sent, "docs", 0, 0, tiled=True)
     spread, lambda_column = pl.pallas_call(
         functools.partial(lambda_kernel, capacity),
-        out_shape=(whole((members, 8, rows), jnp.float32), whole((rows, 1), jnp.float32)),
+        out_shape=(whole((8, rows), jnp.float32), whole((rows, 1), jnp.float32)),
         in_specs=[pl.BlockSpec(memory_space=pltpu.SMEM)] + vmem_specs(2),
         out_specs=tuple(vmem_specs(2)),
         scratch_shapes=[pltpu.VMEM((docs * capacity, LANES), jnp.float32)] * 4
         + [pltpu.VMEM((4 * docs, LANES), jnp.float32)],
         name="lambdas",
-    )(place, got, slot)
-    parities = [list(range(parity, lanes, 2)) for parity in range(2)]
-    all_lambdas = lax.all_to_all(
-        spread, "mp", 0, 0, axis_index_groups=parities, tiled=True
-    )
+    )(place, on_chip(got), slot)
+    gathered = [
+        lax.ppermute(spread, "mp", [(i, (i + by) % lanes) for i in range(lanes)])
+        for by in (lanes // 2, 2, -2)
+    ]
+    across_lambdas, back_lambdas, on_lambdas = (on_chip(x) for x in gathered)
 
     part_rows = width // (lanes * subs)
     targets = 2 * subs
     wide = targets * part_rows
     columns = units // LANES
     prepared = slopes(place, w_first, w2_row, [embeddings, back, on, across], wide)
-    offsets = ((0, members - 1, 1, 2),)
     sent = pl.pallas_call(
-        functools.partial(product_kernel, offsets),
-        out_shape=whole((targets, (part_rows + 1) * columns, LANES), jnp.bfloat16),
-        in_specs=[pl.BlockSpec(memory_space=pltpu.SMEM)] + vmem_specs(4),
+        product_kernel,
+        out_shape=pltpu.VMEM((targets, (part_rows + 1) * columns, LANES), jnp.bfloat16),
+        in_specs=vmem_specs(7),
         out_specs=vmem_specs(1)[0],
         name="product",
-    )(place, all_lambdas, *prepared)
+    )(spread, back_lambdas, on_lambdas, across_lambdas, *prepared)
     cells = [list(range(i, i + targets)) for i in range(0, lanes * subs, targets)]
     arrived = lax.all_to_all(
         sent, ("mp", "sub"), 0, 0, axis_index_groups=cells, tiled=True

time: 145 us -> 164 us (1.13)
  waiting for transfers between devices: 21.5 us -> 38.2 us
  starting transfers between devices: 68.5 us -> 73.5 us
    ppermute x2, waiting for transfers between devices: 0.01 us -> 13.9 us  [moved(): return lax.ppermute(x, 'mp', [(i, (i + by) % lanes) for i in range(lanes)])]
    ppermute x0 -> x3, starting transfers between devices: none -> 11.3 us  [on_device(): lax.ppermute(spread, 'mp', [(i, (i + by) % lanes) for i in range(lanes)])]
    all_to_all x1 -> x0, starting transfers between devices: 6.99 us -> none  [on_device(): lax.all_to_all(spread, 'mp', 0, 0, axis_index_groups=parities, tiled=True)]
    all_to_all x1, waiting for transfers between devices: 7.9 us -> 12.2 us  [on_device(): got = lax.all_to_all(sent, 'docs', 0, 0, tiled=True)]
    all_to_all x1 -> x0, waiting for transfers between devices: 2.18 us -> none  [on_device(): lax.all_to_all(spread, 'mp', 0, 0, axis_index_groups=parities, tiled=True)]
  transfers between devices with their start and end apart: 6 -> 8, of which waited for: 3 -> 5; matrix products, arithmetic and copies ran while one was open for 3% -> 2% of each run, Pallas kernels for 9% -> 8%
where the time goes in v4:
time: 164 us
  starting transfers between devices  73.5 us (45%)
  waiting for transfers between devices  38.2 us (23%)
  blocking collectives  30.1 us (18%)
  Pallas kernels  15 us (9%)
  matrix products  2.48 us (2%)
  local copies, waits for them, and re-layouts  2.01 us (1%)
    all_to_all x1, starting transfers between devices, on_device(): got = lax.all_to_all(sent, 'docs', 0, 0, tiled=True)  43.7 us
    all_to_all x1, blocking collectives, on_device(): lax.all_to_all(jnp.concatenate([tiles, second], axis=1), 'docs', 0, 0, ti...  18.7 us
    ppermute x2, waiting for transfers between devices, moved(): return lax.ppermute(x, 'mp', [(i, (i + by) % lanes) for i in range(lanes)])  13.9 us
    all_to_all x1, waiting for transfers between devices, on_device(): got = lax.all_to_all(sent, 'docs', 0, 0, tiled=True)  12.2 us
    all_to_all x1, blocking collectives, on_device(): lax.all_to_all(sent, ('mp', 'sub'), 0, 0, axis_index_groups=cells, tiled=...  11.5 us
    all_to_all x1, waiting for transfers between devices, sent_to_all(): lax.all_to_all(jnp.broadcast_to(x[None], (count, *x.shape)), axis, 0, 0,...  11.4 us
    ppermute x3, starting transfers between devices, on_device(): lax.ppermute(spread, 'mp', [(i, (i + by) % lanes) for i in range(lanes)])  11.3 us
    ppermute x2, starting transfers between devices, moved(): return lax.ppermute(x, 'mp', [(i, (i + by) % lanes) for i in range(lanes)])  8.45 us
  transfers between devices with their start and end apart: 8, of which 5 were waited for; matrix products, arithmetic and copies ran while one was open for 2% of the time, Pallas kernels for 8%

profile of v4, /device:TPU:80, one launch (start us, length us, event | category | flops | bytes accessed | tf_op | source)
XLA Modules:
  0.0 163.7 jit_solution(1147098174441658856)
XLA Ops:
  0.6 4.6 %collective-permute-start.3 = (bf16[128,1024]{1,0:T(8,128)(2,1)}, bf16[128,1024]{1,0:T(8,128)(2,1)S(1)}, u32[]{:S(2)}, u32[]{:S(2)}) collective-permute-start(bf16[128,1024]{1,0:T(8,128)(2,1)} %refs_0_.1), channel_id=1, source_target_pairs={{0,4},{2,6},{4,8},{6,10},{8,12},{10,14},{12,0},{14,2},{1,5},{3,7},... | collective-permute-start | bytes 786440 | tf_op jit(solution)/shard_map/ppermute | solution.py:234
  5.3 3.8 %collective-permute-start.4 = (bf16[128,1024]{1,0:T(8,128)(2,1)}, bf16[128,1024]{1,0:T(8,128)(2,1)S(1)}, u32[]{:S(2)}, u32[]{:S(2)}) collective-permute-start(bf16[128,1024]{1,0:T(8,128)(2,1)} %refs_0_.1), channel_id=1, source_target_pairs={{0,12},{2,14},{4,0},{6,2},{8,4},{10,6},{12,8},{14,10},{1,13},{3,15... | collective-permute-start | bytes 786440 | tf_op jit(solution)/shard_map/ppermute | solution.py:234
  9.1 7.5 %collective-permute-done.3.refs_1_ = bf16[128,1024]{1,0:T(8,128)(2,1)S(1)} collective-permute-done((bf16[128,1024]{1,0:T(8,128)(2,1)}, bf16[128,1024]{1,0:T(8,128)(2,1)S(1)}, u32[]{:S(2)}, u32[]{:S(2)}) %collective-permute-start.3) | collective-permute-done | bytes 262176 | tf_op jit(solution)/shard_map/ppermute | solution.py:234
  16.6 6.4 %collective-permute-done.4.refs_2_ = bf16[128,1024]{1,0:T(8,128)(2,1)S(1)} collective-permute-done((bf16[128,1024]{1,0:T(8,128)(2,1)}, bf16[128,1024]{1,0:T(8,128)(2,1)S(1)}, u32[]{:S(2)}, u32[]{:S(2)}) %collective-permute-start.4) | collective-permute-done | bytes 262176 | tf_op jit(solution)/shard_map/ppermute | solution.py:234
  23.1 5.2 %collective-permute-start.5 = (bf16[128,1024]{1,0:T(8,128)(2,1)S(1)}, bf16[128,1024]{1,0:T(8,128)(2,1)S(1)}, u32[]{:S(2)}, u32[]{:S(2)}) collective-permute-start(bf16[128,1024]{1,0:T(8,128)(2,1)S(1)} %broadcast_select_fusion), channel_id=1, source_target_pairs={{0,4},{1,13},{2,6},{3,15},{4,8},{5,1},{6,10},{7,3},{8,12},{9,5},{1... | collective-permute-start | bytes 786440 | tf_op jit(solution)/shard_map/ppermute | solution.py:243
  28.3 2.8 %score.1 = (f32[16,8,128]{2,1,0:T(8,128)}, s32[128,1]{1,0:T(8,128)}) custom-call(bf16[128,1024]{1,0:T(8,128)(2,1)} %refs_0_.1, bf16[1024,1024]{1,0:T(8,128)(2,1)} %w1_ref.3, f32[1,1024]{1,0:T(1,128)} %bitcast.28, s32[1,128]{1,0:T(1,128)} %bitcast.30, s32[1,128]{1,0:T(1,128)} %bitcast.31, s32[1,128]{1,0:T(1,128)} %bitcast.32), custom_call_target="tpu_custom_call" | custom-call | tf_op jit(solution)/shard_map/score/pallas_call | solution.py:256
  31.1 43.7 %all-to-all-start = ((f32[16,8,128]{2,1,0:T(8,128)}), f32[16,8,128]{2,1,0:T(8,128)S(1)}, u32[]{:S(2)}, u32[]{:S(2)}) async-start(f32[16,8,128]{2,1,0:T(8,128)} %get-tuple-element.12), calls=%async_computation | async-start | bytes 131072 | tf_op jit(solution)/shard_map/all_to_all | solution.py:269
  75.3 12.2 %all-to-all-done.got_ref = f32[16,8,128]{2,1,0:T(8,128)S(1)} async-done(((f32[16,8,128]{2,1,0:T(8,128)}), f32[16,8,128]{2,1,0:T(8,128)S(1)}, u32[]{:S(2)}, u32[]{:S(2)}) %all-to-all-start) | async-done | bytes 65568 | tf_op jit(solution)/shard_map/all_to_all | solution.py:269
  87.5 4.7 %lambdas.1 = (f32[8,128]{1,0:T(8,128)}, f32[128,1]{1,0:T(8,128)}) custom-call(s32[3]{0:T(128)} %pad_add_fusion.place_ref, f32[16,8,128]{2,1,0:T(8,128)S(1)} %all-to-all-done.got_ref, s32[128,1]{1,0:T(8,128)} %get-tuple-element.13.slot_ref), custom_call_target="tpu_custom_call" | custom-call | tf_op jit(solution)/shard_map/lambdas/pallas_call | solution.py:270
  92.2 2.2 %collective-permute-start = (f32[8,128]{1,0:T(8,128)}, f32[8,128]{1,0:T(8,128)S(1)}, u32[]{:S(2)}, u32[]{:S(2)}) collective-permute-start(f32[8,128]{1,0:T(8,128)} %get-tuple-element.15.refs_0_), channel_id=1, source_target_pairs={{0,4},{2,6},{4,8},{6,10},{8,12},{10,14},{12,0},{14,2},{1,5},{3,7},... | collective-permute-start | bytes 12296 | tf_op jit(solution)/shard_map/ppermute | solution.py:280
  94.4 5.8 %collective-permute-start.1 = (f32[8,128]{1,0:T(8,128)}, f32[8,128]{1,0:T(8,128)S(1)}, u32[]{:S(2)}, u32[]{:S(2)}) collective-permute-start(f32[8,128]{1,0:T(8,128)} %get-tuple-element.15.refs_0_), channel_id=1, source_target_pairs={{0,12},{2,14},{4,0},{6,2},{8,4},{10,6},{12,8},{14,10},{1,13},{3,15... | collective-permute-start | bytes 12296 | tf_op jit(solution)/shard_map/ppermute | solution.py:280
  100.2 3.3 %collective-permute-start.2 = (f32[8,128]{1,0:T(8,128)}, f32[8,128]{1,0:T(8,128)S(1)}, u32[]{:S(2)}, u32[]{:S(2)}) collective-permute-start(f32[8,128]{1,0:T(8,128)} %get-tuple-element.15.refs_0_), channel_id=1, source_target_pairs={{0,8},{2,10},{4,12},{6,14},{8,0},{10,2},{12,4},{14,6},{1,9},{3,11}... | collective-permute-start | bytes 12296 | tf_op jit(solution)/shard_map/ppermute | solution.py:280
  103.5 0.7 copy-done.3
  104.2 4.9 %slopes.1 = (bf16[4,128,1024]{2,1,0:T(8,128)(2,1)}, bf16[4,128,1024]{2,1,0:T(8,128)(2,1)}, bf16[4,128,256]{2,1,0:T(8,128)(2,1)}) custom-call(s32[3]{0:T(128)} %pad_add_fusion.place_ref, bf16[1024,1024]{1,0:T(8,128)(2,1)} %w1_ref.3, f32[1,1024]{1,0:T(1,128)} %bitcast.29, bf16[128,1024]{1,0:T(8,128)(2,1)} %refs_0_.1, bf16[128,1024]{1,0:T(8,128)(2,1)} %copy-done.1, ...), custom_call_target="tpu_custom_call" | custom-call | tf_op jit(solution)/shard_map/slopes/pallas_call | solution.py:177
  109.1 0.7 collective-permute-done.2.refs_3_
  109.8 2.6 %product.1 = bf16[4,520,128]{2,1,0:T(8,128)(2,1)S(1)} custom-call(f32[8,128]{1,0:T(8,128)} %get-tuple-element.15.refs_0_, f32[8,128]{1,0:T(8,128)S(1)} %collective-permute-done.refs_1_, f32[8,128]{1,0:T(8,128)S(1)} %collective-permute-done.1.refs_2_, f32[8,128]{1,0:T(8,128)S(1)} %collective-permute-done.2.refs_3_, ...), custom_call_target="tpu_custom_call" | custom-call | tf_op jit(solution)/shard_map/product/pallas_call | solution.py:290
  112.5 11.5 %all_to_all.20 = bf16[4,520,128]{2,1,0:T(8,128)(2,1)S(1)} all-to-all(bf16[4,520,128]{2,1,0:T(8,128)(2,1)S(1)} %product.1), channel_id=1, replica_groups={{0,1,2,3},{4,5,6,7},{8,9,10,11},{12,13,14,15},{16,17,18,19},{20,21,22,2..., dimensions={0} | all-to-all | bytes 1064960 | tf_op jit(solution)/shard_map/all_to_all | solution.py:298
  124.1 18.7 %all_to_all.21 = bf16[16,40,128]{2,1,0:T(8,128)(2,1)S(1)} all-to-all(bf16[16,40,128]{2,1,0:T(8,128)(2,1)S(1)} %pad_maximum_fusion), channel_id=1, replica_groups=mesh['groups'=2,'docs'=16,'mp'=8,'sub'=2] {'docs'}, dimensions={0} | all-to-all | bytes 327680 | tf_op jit(solution)/shard_map/all_to_all | solution.py:305
  142.8 0.7 broadcast_in_dim.5
  143.5 4.9 %all-to-all-start.3 = ((bf16[16,32,128]{2,1,0:T(8,128)(2,1)}), bf16[16,32,128]{2,1,0:T(8,128)(2,1)S(1)}, u32[]{:S(2)}, u32[]{:S(2)}) async-start(bf16[16,32,128]{2,1,0:T(8,128)(2,1)} %broadcast_in_dim.5), calls=%async_computation.3 | async-start | bytes 262144 | tf_op jit(solution)/shard_map/all_to_all | solution.py:227
  148.5 0.6 slice_bitcast_fusion
  149.1 2.5 %fusion = bf16[128,1024]{1,0:T(8,128)(2,1)} fusion(bf16[1024,1024]{1,0:T(8,128)(2,1)S(1)} %copy-done, bf16[4,128,1024]{2,1,0:T(8,128)(2,1)} %get-tuple-element.16.refs_4_, f32[128]{0:T(128)S(1)} %reduce.1), kind=kOutput, calls=%fused_computation.1 | convolution fusion | flops 268697600 | bytes 2621952 | tf_op jit(solution)/shard_map/dot_general | solution.py:308
  151.6 11.4 %all-to-all-done.3 = bf16[16,32,128]{2,1,0:T(8,128)(2,1)S(1)} async-done(((bf16[16,32,128]{2,1,0:T(8,128)(2,1)}), bf16[16,32,128]{2,1,0:T(8,128)(2,1)S(1)}, u32[]{:S(2)}, u32[]{:S(2)}) %all-to-all-start.3) | async-done | bytes 131104 | tf_op jit(solution)/shard_map/all_to_all | solution.py:227
  163.0 0.7 copy_bitcast_fusion
  (22 shorter events, 0.9 us)
Async XLA Ops:
  0.6 16.0 %collective-permute-start.3 = (bf16[128,1024]{1,0:T(8,128)(2,1)}, bf16[128,1024]{1,0:T(8,128)(2,1)S(1)}, u32[]{:S(2)}, u32[]{:S(2)}) collective-permute-start(bf16[128,1024]{1,0:T(8,128)(2,1)} %refs_0_.1), channel_id=1, source_target_pairs={{0,4},{2,6},{4,8},{6,10},{8,12},{10,14},{12,0},{14,2},{1,5},{3,7},... | collective-permute-start | bytes 786440 | tf_op jit(solution)/shard_map/ppermute | solution.py:234
  5.3 17.8 %collective-permute-start.4 = (bf16[128,1024]{1,0:T(8,128)(2,1)}, bf16[128,1024]{1,0:T(8,128)(2,1)S(1)}, u32[]{:S(2)}, u32[]{:S(2)}) collective-permute-start(bf16[128,1024]{1,0:T(8,128)(2,1)} %refs_0_.1), channel_id=1, source_target_pairs={{0,12},{2,14},{4,0},{6,2},{8,4},{10,6},{12,8},{14,10},{1,13},{3,15... | collective-permute-start | bytes 786440 | tf_op jit(solution)/shard_map/ppermute | solution.py:234
  16.6 86.8 %copy-start.1 = (bf16[128,1024]{1,0:T(8,128)(2,1)}, bf16[128,1024]{1,0:T(8,128)(2,1)S(1)}, u32[]{:S(2)}) copy-start(bf16[128,1024]{1,0:T(8,128)(2,1)S(1)} %collective-permute-done.3.refs_1_) | copy-start | bytes 786436
  23.0 80.5 %copy-start.2 = (bf16[128,1024]{1,0:T(8,128)(2,1)}, bf16[128,1024]{1,0:T(8,128)(2,1)S(1)}, u32[]{:S(2)}) copy-start(bf16[128,1024]{1,0:T(8,128)(2,1)S(1)} %collective-permute-done.4.refs_2_) | copy-start | bytes 786436
  23.1 80.4 %collective-permute-start.5 = (bf16[128,1024]{1,0:T(8,128)(2,1)S(1)}, bf16[128,1024]{1,0:T(8,128)(2,1)S(1)}, u32[]{:S(2)}, u32[]{:S(2)}) collective-permute-start(bf16[128,1024]{1,0:T(8,128)(2,1)S(1)} %broadcast_select_fusion), channel_id=1, source_target_pairs={{0,4},{1,13},{2,6},{3,15},{4,8},{5,1},{6,10},{7,3},{8,12},{9,5},{1... | collective-permute-start | bytes 786440 | tf_op jit(solution)/shard_map/ppermute | solution.py:243
  31.1 56.4 %all-to-all-start = ((f32[16,8,128]{2,1,0:T(8,128)}), f32[16,8,128]{2,1,0:T(8,128)S(1)}, u32[]{:S(2)}, u32[]{:S(2)}) async-start(f32[16,8,128]{2,1,0:T(8,128)} %get-tuple-element.12), calls=%async_computation | async-start | bytes 131072 | tf_op jit(solution)/shard_map/all_to_all | solution.py:269
  92.2 16.9 %collective-permute-start = (f32[8,128]{1,0:T(8,128)}, f32[8,128]{1,0:T(8,128)S(1)}, u32[]{:S(2)}, u32[]{:S(2)}) collective-permute-start(f32[8,128]{1,0:T(8,128)} %get-tuple-element.15.refs_0_), channel_id=1, source_target_pairs={{0,4},{2,6},{4,8},{6,10},{8,12},{10,14},{12,0},{14,2},{1,5},{3,7},... | collective-permute-start | bytes 12296 | tf_op jit(solution)/shard_map/ppermute | solution.py:280
  94.4 14.7 %collective-permute-start.1 = (f32[8,128]{1,0:T(8,128)}, f32[8,128]{1,0:T(8,128)S(1)}, u32[]{:S(2)}, u32[]{:S(2)}) collective-permute-start(f32[8,128]{1,0:T(8,128)} %get-tuple-element.15.refs_0_), channel_id=1, source_target_pairs={{0,12},{2,14},{4,0},{6,2},{8,4},{10,6},{12,8},{14,10},{1,13},{3,15... | collective-permute-start | bytes 12296 | tf_op jit(solution)/shard_map/ppermute | solution.py:280
  100.2 9.6 %collective-permute-start.2 = (f32[8,128]{1,0:T(8,128)}, f32[8,128]{1,0:T(8,128)S(1)}, u32[]{:S(2)}, u32[]{:S(2)}) collective-permute-start(f32[8,128]{1,0:T(8,128)} %get-tuple-element.15.refs_0_), channel_id=1, source_target_pairs={{0,8},{2,10},{4,12},{6,14},{8,0},{10,2},{12,4},{14,6},{1,9},{3,11}... | collective-permute-start | bytes 12296 | tf_op jit(solution)/shard_map/ppermute | solution.py:280
  103.5 0.7 copy-start.3
  112.5 35.9 %copy-start.4 = (f32[128,1]{1,0:T(8,128)S(1)}, f32[128,1]{1,0:T(8,128)}, u32[]{:S(2)}) copy-start(f32[128,1]{1,0:T(8,128)} %get-tuple-element.19) | copy-start | bytes 1540
  112.5 36.6 %copy-start = (bf16[1024,1024]{1,0:T(8,128)(2,1)S(1)}, bf16[1024,1024]{1,0:T(8,128)(2,1)}, u32[]{:S(2)}) copy-start(bf16[1024,1024]{1,0:T(8,128)(2,1)} %w1_ref.3) | copy-start | bytes 6291460
  143.5 19.5 %all-to-all-start.3 = ((bf16[16,32,128]{2,1,0:T(8,128)(2,1)}), bf16[16,32,128]{2,1,0:T(8,128)(2,1)S(1)}, u32[]{:S(2)}, u32[]{:S(2)}) async-start(bf16[16,32,128]{2,1,0:T(8,128)(2,1)} %broadcast_in_dim.5), calls=%async_computation.3 | async-start | bytes 262144 | tf_op jit(solution)/shard_map/all_to_all | solution.py:227

commit v5 on v1

--- a/solution.py
+++ b/solution.py
@@ -13,6 +13,10 @@
 
 def whole(*shape_and_type):
     return jax.ShapeDtypeStruct(*shape_and_type)
+
+
+def on_chip(x):
+    return pltpu.with_memory_space_constraint(x, pltpu.VMEM)
 
 
 def vmem_specs(count):
@@ -275,7 +279,7 @@
         scratch_shapes=[pltpu.VMEM((docs * capacity, LANES), jnp.float32)] * 4
         + [pltpu.VMEM((4 * docs, LANES), jnp.float32)],
         name="lambdas",
-    )(place, got, slot)
+    )(place, on_chip(got), slot)
     parities = [list(range(parity, lanes, 2)) for parity in range(2)]
     all_lambdas = lax.all_to_all(
         spread, "mp", 0, 0, axis_index_groups=parities, tiled=True
@@ -289,11 +293,11 @@
     offsets = ((0, members - 1, 1, 2),)
     sent = pl.pallas_call(
         functools.partial(product_kernel, offsets),
-        out_shape=whole((targets, (part_rows + 1) * columns, LANES), jnp.bfloat16),
+        out_shape=pltpu.VMEM((targets, (part_rows + 1) * columns, LANES), jnp.bfloat16),
         in_specs=[pl.BlockSpec(memory_space=pltpu.SMEM)] + vmem_specs(4),
         out_specs=vmem_specs(1)[0],
         name="product",
-    )(place, all_lambdas, *prepared)
+    )(place, on_chip(all_lambdas), *prepared)
     cells = [list(range(i, i + targets)) for i in range(0, lanes * subs, targets)]
     arrived = lax.all_to_all(
         sent, ("mp", "sub"), 0, 0, axis_index_groups=cells, tiled=True

time: 145 us -> 142 us (0.979)
  no operation moved by 1% of the time
where the time goes in v5:
time: 142 us; the launch traced here: 141 us
  starting transfers between devices  68.6 us (48%)
  blocking collectives  29.3 us (21%)
  waiting for transfers between devices  21.5 us (15%)
  Pallas kernels  15 us (11%)
  matrix products  2.48 us (2%)
  local copies, waits for them, and re-layouts  2.02 us (1%)
  other arithmetic  1.53 us (1%)
    all_to_all x1, starting transfers between devices, on_device(): got = lax.all_to_all(sent, 'docs', 0, 0, tiled=True)  43.7 us
    all_to_all x1, blocking collectives, on_device(): lax.all_to_all(jnp.concatenate([tiles, second], axis=1), 'docs', 0, 0, ti...  17.8 us
    all_to_all x1, blocking collectives, on_device(): lax.all_to_all(sent, ('mp', 'sub'), 0, 0, axis_index_groups=cells, tiled=...  11.5 us
    all_to_all x1, waiting for transfers between devices, sent_to_all(): lax.all_to_all(jnp.broadcast_to(x[None], (count, *x.shape)), axis, 0, 0,...  11.4 us
    ppermute x2, starting transfers between devices, moved(): return lax.ppermute(x, 'mp', [(i, (i + by) % lanes) for i in range(lanes)])  8.45 us
    all_to_all x1, waiting for transfers between devices, on_device(): got = lax.all_to_all(sent, 'docs', 0, 0, tiled=True)  7.9 us
    all_to_all x1, starting transfers between devices, on_device(): lax.all_to_all(spread, 'mp', 0, 0, axis_index_groups=parities, tiled=True)  6.99 us
    all_to_all x1, starting transfers between devices, sent_to_all(): lax.all_to_all(jnp.broadcast_to(x[None], (count, *x.shape)), axis, 0, 0,...  5.5 us
  transfers between devices with their start and end apart: 6, of which 3 were waited for; matrix products, arithmetic and copies ran while one was open for 3% of the time, Pallas kernels for 9%

profile of v5, /device:TPU:80, one launch (start us, length us, event | category | flops | bytes accessed | tf_op | source)
XLA Modules:
  0.0 141.3 jit_solution(16764659444938349616)
XLA Ops:
  0.6 4.6 %collective-permute-start = (bf16[128,1024]{1,0:T(8,128)(2,1)}, bf16[128,1024]{1,0:T(8,128)(2,1)S(1)}, u32[]{:S(2)}, u32[]{:S(2)}) collective-permute-start(bf16[128,1024]{1,0:T(8,128)(2,1)} %refs_0_.1), channel_id=1, source_target_pairs={{0,4},{2,6},{4,8},{6,10},{8,12},{10,14},{12,0},{14,2},{1,5},{3,7},... | collective-permute-start | bytes 786440 | tf_op jit(solution)/shard_map/ppermute | solution.py:237
  5.3 3.8 %collective-permute-start.1 = (bf16[128,1024]{1,0:T(8,128)(2,1)}, bf16[128,1024]{1,0:T(8,128)(2,1)S(1)}, u32[]{:S(2)}, u32[]{:S(2)}) collective-permute-start(bf16[128,1024]{1,0:T(8,128)(2,1)} %refs_0_.1), channel_id=1, source_target_pairs={{0,12},{2,14},{4,0},{6,2},{8,4},{10,6},{12,8},{14,10},{1,13},{3,15... | collective-permute-start | bytes 786440 | tf_op jit(solution)/shard_map/ppermute | solution.py:237
  9.1 2.8 %score.1 = (f32[16,8,128]{2,1,0:T(8,128)}, s32[128,1]{1,0:T(8,128)}) custom-call(bf16[128,1024]{1,0:T(8,128)(2,1)} %refs_0_.1, bf16[1024,1024]{1,0:T(8,128)(2,1)} %w1_ref.3, f32[1,1024]{1,0:T(1,128)} %bitcast.28, s32[1,128]{1,0:T(1,128)} %bitcast.30, s32[1,128]{1,0:T(1,128)} %bitcast.31, s32[1,128]{1,0:T(1,128)} %bitcast.32), custom_call_target="tpu_custom_call" | custom-call | tf_op jit(solution)/shard_map/score/pallas_call | solution.py:260
  11.9 43.7 %all-to-all-start = ((f32[16,8,128]{2,1,0:T(8,128)}), f32[16,8,128]{2,1,0:T(8,128)S(1)}, u32[]{:S(2)}, u32[]{:S(2)}) async-start(f32[16,8,128]{2,1,0:T(8,128)} %get-tuple-element.12), calls=%async_computation | async-start | bytes 131072 | tf_op jit(solution)/shard_map/all_to_all | solution.py:273
  55.6 0.0 copy-start.1
  55.7 4.0 %collective-permute-start.2 = (bf16[128,1024]{1,0:T(8,128)(2,1)S(1)}, bf16[128,1024]{1,0:T(8,128)(2,1)S(1)}, u32[]{:S(2)}, u32[]{:S(2)}) collective-permute-start(bf16[128,1024]{1,0:T(8,128)(2,1)S(1)} %broadcast_select_fusion), channel_id=1, source_target_pairs={{0,4},{1,13},{2,6},{3,15},{4,8},{5,1},{6,10},{7,3},{8,12},{9,5},{1... | collective-permute-start | bytes 786440 | tf_op jit(solution)/shard_map/ppermute | solution.py:246
  59.7 0.6 pad_add_fusion.place_ref
  60.2 7.9 %all-to-all-done.got_ref = f32[16,8,128]{2,1,0:T(8,128)S(1)} async-done(((f32[16,8,128]{2,1,0:T(8,128)}), f32[16,8,128]{2,1,0:T(8,128)S(1)}, u32[]{:S(2)}, u32[]{:S(2)}) %all-to-all-start) | async-done | bytes 65568 | tf_op jit(solution)/shard_map/all_to_all | solution.py:273
  68.1 4.7 %lambdas.1 = (f32[4,8,128]{2,1,0:T(8,128)}, f32[128,1]{1,0:T(8,128)}) custom-call(s32[3]{0:T(128)} %pad_add_fusion.place_ref, f32[16,8,128]{2,1,0:T(8,128)S(1)} %all-to-all-done.got_ref, s32[128,1]{1,0:T(8,128)} %get-tuple-element.13.slot_ref), custom_call_target="tpu_custom_call" | custom-call | tf_op jit(solution)/shard_map/lambdas/pallas_call | solution.py:274
  72.8 7.0 %all-to-all-start.1 = ((f32[4,8,128]{2,1,0:T(8,128)}), f32[4,8,128]{2,1,0:T(8,128)S(1)}, u32[]{:S(2)}, u32[]{:S(2)}) async-start(f32[4,8,128]{2,1,0:T(8,128)} %get-tuple-element.15), calls=%async_computation.1 | async-start | bytes 32768 | tf_op jit(solution)/shard_map/all_to_all | solution.py:284
  79.8 0.7 copy-done.3
  80.5 4.9 %slopes.1 = (bf16[4,128,1024]{2,1,0:T(8,128)(2,1)}, bf16[4,128,1024]{2,1,0:T(8,128)(2,1)}, bf16[4,128,256]{2,1,0:T(8,128)(2,1)}) custom-call(s32[3]{0:T(128)} %pad_add_fusion.place_ref, bf16[1024,1024]{1,0:T(8,128)(2,1)} %w1_ref.3, f32[1,1024]{1,0:T(1,128)} %bitcast.29, bf16[128,1024]{1,0:T(8,128)(2,1)} %refs_0_.1, bf16[128,1024]{1,0:T(8,128)(2,1)} %copy-done.1, ...), custom_call_target="tpu_custom_call" | custom-call | tf_op jit(solution)/shard_map/slopes/pallas_call | solution.py:177
  85.4 2.1 %all-to-all-done.1.lambda_ref = f32[4,8,128]{2,1,0:T(8,128)S(1)} async-done(((f32[4,8,128]{2,1,0:T(8,128)}), f32[4,8,128]{2,1,0:T(8,128)S(1)}, u32[]{:S(2)}, u32[]{:S(2)}) %all-to-all-start.1) | async-done | bytes 16416 | tf_op jit(solution)/shard_map/all_to_all | solution.py:284
  87.6 2.6 %product.1 = bf16[4,520,128]{2,1,0:T(8,128)(2,1)S(1)} custom-call(s32[3]{0:T(128)} %pad_add_fusion.place_ref, f32[4,8,128]{2,1,0:T(8,128)S(1)} %all-to-all-done.1.lambda_ref, bf16[4,128,1024]{2,1,0:T(8,128)(2,1)} %get-tuple-element.16.refs_0_, bf16[4,128,1024]{2,1,0:T(8,128)(2,1)} %get-tuple-element.17.refs_1_, bf16[4,128,256]{2,1,0:T(8,128)(2,1)} %get-tuple-element.18.refs_2_), custom_call_target="tpu_custom_call" | custom-call | tf_op jit(solution)/shard_map/product/pallas_call | solution.py:294
  90.2 11.5 %all_to_all.25 = bf16[4,520,128]{2,1,0:T(8,128)(2,1)S(1)} all-to-all(bf16[4,520,128]{2,1,0:T(8,128)(2,1)S(1)} %product.1), channel_id=1, replica_groups={{0,1,2,3},{4,5,6,7},{8,9,10,11},{12,13,14,15},{16,17,18,19},{20,21,22,2..., dimensions={0} | all-to-all | bytes 1064960 | tf_op jit(solution)/shard_map/all_to_all | solution.py:302
  101.7 0.1 reduce_sum.21
  101.9 17.8 %all_to_all.26 = bf16[16,40,128]{2,1,0:T(8,128)(2,1)S(1)} all-to-all(bf16[16,40,128]{2,1,0:T(8,128)(2,1)S(1)} %pad_maximum_fusion), channel_id=1, replica_groups=mesh['groups'=2,'docs'=16,'mp'=8,'sub'=2] {'docs'}, dimensions={0} | all-to-all | bytes 327680 | tf_op jit(solution)/shard_map/all_to_all | solution.py:309
  119.8 0.7 broadcast_in_dim.5
  120.4 5.5 %all-to-all-start.4 = ((bf16[16,32,128]{2,1,0:T(8,128)(2,1)}), bf16[16,32,128]{2,1,0:T(8,128)(2,1)S(1)}, u32[]{:S(2)}, u32[]{:S(2)}) async-start(bf16[16,32,128]{2,1,0:T(8,128)(2,1)} %broadcast_in_dim.5), calls=%async_computation.4 | async-start | bytes 262144 | tf_op jit(solution)/shard_map/all_to_all | solution.py:230
  125.9 0.1 reduce.1
  126.1 0.6 slice_bitcast_fusion
  126.7 2.5 %fusion = bf16[128,1024]{1,0:T(8,128)(2,1)} fusion(bf16[1024,1024]{1,0:T(8,128)(2,1)S(1)} %copy-done, bf16[4,128,1024]{2,1,0:T(8,128)(2,1)} %get-tuple-element.16.refs_0_, f32[128]{0:T(128)S(1)} %reduce.1), kind=kOutput, calls=%fused_computation.1 | convolution fusion | flops 268697600 | bytes 2621952 | tf_op jit(solution)/shard_map/dot_general | solution.py:312
  129.1 11.4 %all-to-all-done.4 = bf16[16,32,128]{2,1,0:T(8,128)(2,1)S(1)} async-done(((bf16[16,32,128]{2,1,0:T(8,128)(2,1)}), bf16[16,32,128]{2,1,0:T(8,128)(2,1)S(1)}, u32[]{:S(2)}, u32[]{:S(2)}) %all-to-all-start.4) | async-done | bytes 131104 | tf_op jit(solution)/shard_map/all_to_all | solution.py:230
  140.6 0.7 copy_bitcast_fusion
  (18 shorter events, 0.1 us)
Async XLA Ops:
  0.6 55.0 %collective-permute-start = (bf16[128,1024]{1,0:T(8,128)(2,1)}, bf16[128,1024]{1,0:T(8,128)(2,1)S(1)}, u32[]{:S(2)}, u32[]{:S(2)}) collective-permute-start(bf16[128,1024]{1,0:T(8,128)(2,1)} %refs_0_.1), channel_id=1, source_target_pairs={{0,4},{2,6},{4,8},{6,10},{8,12},{10,14},{12,0},{14,2},{1,5},{3,7},... | collective-permute-start | bytes 786440 | tf_op jit(solution)/shard_map/ppermute | solution.py:237
  5.3 50.4 %collective-permute-start.1 = (bf16[128,1024]{1,0:T(8,128)(2,1)}, bf16[128,1024]{1,0:T(8,128)(2,1)S(1)}, u32[]{:S(2)}, u32[]{:S(2)}) collective-permute-start(bf16[128,1024]{1,0:T(8,128)(2,1)} %refs_0_.1), channel_id=1, source_target_pairs={{0,12},{2,14},{4,0},{6,2},{8,4},{10,6},{12,8},{14,10},{1,13},{3,15... | collective-permute-start | bytes 786440 | tf_op jit(solution)/shard_map/ppermute | solution.py:237
  11.9 56.2 %all-to-all-start = ((f32[16,8,128]{2,1,0:T(8,128)}), f32[16,8,128]{2,1,0:T(8,128)S(1)}, u32[]{:S(2)}, u32[]{:S(2)}) async-start(f32[16,8,128]{2,1,0:T(8,128)} %get-tuple-element.12), calls=%async_computation | async-start | bytes 131072 | tf_op jit(solution)/shard_map/all_to_all | solution.py:273
  55.6 24.2 %copy-start.1 = (bf16[128,1024]{1,0:T(8,128)(2,1)}, bf16[128,1024]{1,0:T(8,128)(2,1)S(1)}, u32[]{:S(2)}) copy-start(bf16[128,1024]{1,0:T(8,128)(2,1)S(1)} %collective-permute-done.refs_1_) | copy-start | bytes 786436
  55.6 24.2 %copy-start.2 = (bf16[128,1024]{1,0:T(8,128)(2,1)}, bf16[128,1024]{1,0:T(8,128)(2,1)S(1)}, u32[]{:S(2)}) copy-start(bf16[128,1024]{1,0:T(8,128)(2,1)S(1)} %collective-permute-done.1.refs_2_) | copy-start | bytes 786436
  55.7 24.1 %collective-permute-start.2 = (bf16[128,1024]{1,0:T(8,128)(2,1)S(1)}, bf16[128,1024]{1,0:T(8,128)(2,1)S(1)}, u32[]{:S(2)}, u32[]{:S(2)}) collective-permute-start(bf16[128,1024]{1,0:T(8,128)(2,1)S(1)} %broadcast_select_fusion), channel_id=1, source_target_pairs={{0,4},{1,13},{2,6},{3,15},{4,8},{5,1},{6,10},{7,3},{8,12},{9,5},{1... | collective-permute-start | bytes 786440 | tf_op jit(solution)/shard_map/ppermute | solution.py:246
  72.8 14.8 %all-to-all-start.1 = ((f32[4,8,128]{2,1,0:T(8,128)}), f32[4,8,128]{2,1,0:T(8,128)S(1)}, u32[]{:S(2)}, u32[]{:S(2)}) async-start(f32[4,8,128]{2,1,0:T(8,128)} %get-tuple-element.15), calls=%async_computation.1 | async-start | bytes 32768 | tf_op jit(solution)/shard_map/all_to_all | solution.py:284
  79.8 0.7 copy-start.3
  90.2 35.7 %copy-start.4 = (f32[128,1]{1,0:T(8,128)S(1)}, f32[128,1]{1,0:T(8,128)}, u32[]{:S(2)}) copy-start(f32[128,1]{1,0:T(8,128)} %get-tuple-element.19) | copy-start | bytes 1540
  90.2 36.4 %copy-start = (bf16[1024,1024]{1,0:T(8,128)(2,1)S(1)}, bf16[1024,1024]{1,0:T(8,128)(2,1)}, u32[]{:S(2)}) copy-start(bf16[1024,1024]{1,0:T(8,128)(2,1)} %w1_ref.3) | copy-start | bytes 6291460
  120.4 20.1 %all-to-all-start.4 = ((bf16[16,32,128]{2,1,0:T(8,128)(2,1)}), bf16[16,32,128]{2,1,0:T(8,128)(2,1)S(1)}, u32[]{:S(2)}, u32[]{:S(2)}) async-start(bf16[16,32,128]{2,1,0:T(8,128)(2,1)} %broadcast_in_dim.5), calls=%async_computation.4 | async-start | bytes 262144 | tf_op jit(solution)/shard_map/all_to_all | solution.py:230

commit v6 on v5

--- a/solution.py
+++ b/solution.py
@@ -91,35 +91,43 @@
     lane = lax.broadcasted_iota(jnp.int32, (sources, LANES), 1)
     position = (source * capacity + lane % capacity).astype(jnp.float32)
     slots = float(sources * capacity)
+    trip = 2 * sources
     lane_of_row = lax.broadcasted_iota(jnp.int32, (rows, LANES), 1)
     lambda_column = jnp.zeros((rows, 1), jnp.float32)
     for h in range(halves):
         half_score = got_ref[:, h, :] * 0.5
         mark = got_ref[:, halves + h, :]
         label = got_ref[:, 2 * halves + h, :]
-        key = label * slots - position
+        key = (label + 8.0 * mark) * slots - position
+        counts = []
+        for query in range(2):
+            here = jnp.sum(jnp.where(mark == query + 1.0, 1.0, 0.0), axis=0, keepdims=True)
+            counts.append(group_sum(jnp.broadcast_to(here, (8, LANES)), capacity)[:1, :])
+        first, other = counts
+        fellows = jnp.where(mark == 1.0, first, jnp.where(mark == 2.0, other, slots - first - other))
+        above = jnp.where(mark == 1.0, other, jnp.where(mark == 2.0, 0.0, first + other))
         for ref, value in ((score_by, half_score), (mark_by, mark), (key_by, key)):
             for c, spread in enumerate(within_groups(value, capacity)):
                 ref[c * sources : (c + 1) * sources, :] = spread
 
         def rank_step(step, sums):
             soft, ideal = sums
-            base = pl.multiple_of(step * 8, 8)
-            score_rows = score_by[pl.ds(base, 8), :]
-            mark_rows = mark_by[pl.ds(base, 8), :]
-            key_rows = key_by[pl.ds(base, 8), :]
-            for r in range(8):
+            base = pl.multiple_of(step * trip, trip)
+            score_rows = score_by[pl.ds(base, trip), :]
+            mark_rows = mark_by[pl.ds(base, trip), :]
+            key_rows = key_by[pl.ds(base, trip), :]
+            for r in range(trip):
                 same = mark_rows[r : r + 1, :] == mark
                 tilt = jnp.tanh(score_rows[r : r + 1, :] - half_score)
-                soft = soft + jnp.where(same, tilt + 1.0, 0.0)
-                ideal = ideal + jnp.where(same & (key_rows[r : r + 1, :] > key), 1.0, 0.0)
+                soft = soft + jnp.where(same, tilt, 0.0)
+                ideal = ideal + jnp.where(key_rows[r : r + 1, :] > key, 1.0, 0.0)
             return soft, ideal
 
         nothing = jnp.zeros((sources, LANES), jnp.float32)
-        soft, ideal = lax.fori_loop(0, capacity * sources // 8, rank_step, (nothing, nothing))
-        discount = 1.0 / jnp.log2(2.0 + (0.5 * soft - 0.5))
+        soft, ideal = lax.fori_loop(0, capacity * sources // trip, rank_step, (nothing, nothing))
+        discount = 1.0 / jnp.log2(2.0 + (0.5 * (soft + fellows) - 0.5))
         gain = jnp.exp2(label) - 1.0
-        term = gain / jnp.log2(2.0 + ideal)
+        term = gain / jnp.log2(2.0 + (ideal - above))
         for c, spread in enumerate(within_groups(discount, capacity)):
             disc_by[c * sources : (c + 1) * sources, :] = spread
 
@@ -139,7 +147,8 @@
         total = jnp.zeros((sources, LANES), jnp.float32)
         for c in range(capacity):
             at = slice(c * sources, (c + 1) * sources)
-            their_gain = jnp.exp2(jnp.ceil(key_by[at, :] * (1.0 / slots))) - 1.0
+            their_label = jnp.ceil(key_by[at, :] * (1.0 / slots)) - 8.0 * mark_by[at, :]
+            their_gain = jnp.exp2(their_label) - 1.0
             gain_gap = own_gain - their_gain
             gap = 2.0 * (score_by[at, :] - own_score)
             pull = jax.nn.sigmoid(jnp.where(gain_gap > 0.0, gap, -gap))

time: 142 us -> 141 us (level)
  transfers between devices with their start and end apart: 6 -> 6, of which waited for: 3 -> 3; matrix products, arithmetic and copies ran while one was open for 3% -> 3% of each run, Pallas kernels for 9% -> 8%
where the time goes in v6:
time: 141 us
  starting transfers between devices  68.5 us (49%)
  blocking collectives  29.4 us (21%)
  waiting for transfers between devices  21.4 us (15%)
  Pallas kernels  14.4 us (10%)
  matrix products  2.48 us (2%)
  local copies, waits for them, and re-layouts  2.02 us (1%)
  other arithmetic  1.53 us (1%)
    all_to_all x1, starting transfers between devices, on_device(): got = lax.all_to_all(sent, 'docs', 0, 0, tiled=True)  43.7 us
    all_to_all x1, blocking collectives, on_device(): lax.all_to_all(jnp.concatenate([tiles, second], axis=1), 'docs', 0, 0, ti...  17.9 us
    all_to_all x1, blocking collectives, on_device(): lax.all_to_all(sent, ('mp', 'sub'), 0, 0, axis_index_groups=cells, tiled=...  11.5 us
    all_to_all x1, waiting for transfers between devices, sent_to_all(): lax.all_to_all(jnp.broadcast_to(x[None], (count, *x.shape)), axis, 0, 0,...  11.4 us
    ppermute x2, starting transfers between devices, moved(): return lax.ppermute(x, 'mp', [(i, (i + by) % lanes) for i in range(lanes)])  8.45 us
    all_to_all x1, waiting for transfers between devices, on_device(): got = lax.all_to_all(sent, 'docs', 0, 0, tiled=True)  7.9 us
    all_to_all x1, starting transfers between devices, on_device(): lax.all_to_all(spread, 'mp', 0, 0, axis_index_groups=parities, tiled=True)  6.99 us
    all_to_all x1, starting transfers between devices, sent_to_all(): lax.all_to_all(jnp.broadcast_to(x[None], (count, *x.shape)), axis, 0, 0,...  5.41 us
  transfers between devices with their start and end apart: 6, of which 3 were waited for; matrix products, arithmetic and copies ran while one was open for 3% of the time, Pallas kernels for 8%

profile of v6, /device:TPU:80, one launch (start us, length us, event | category | flops | bytes accessed | tf_op | source)
XLA Modules:
  0.0 140.7 jit_solution(1323976564855109647)
XLA Ops:
  0.6 4.6 %collective-permute-start = (bf16[128,1024]{1,0:T(8,128)(2,1)}, bf16[128,1024]{1,0:T(8,128)(2,1)S(1)}, u32[]{:S(2)}, u32[]{:S(2)}) collective-permute-start(bf16[128,1024]{1,0:T(8,128)(2,1)} %refs_0_.1), channel_id=1, source_target_pairs={{0,4},{2,6},{4,8},{6,10},{8,12},{10,14},{12,0},{14,2},{1,5},{3,7},... | collective-permute-start | bytes 786440 | tf_op jit(solution)/shard_map/ppermute | solution.py:246
  5.3 3.8 %collective-permute-start.1 = (bf16[128,1024]{1,0:T(8,128)(2,1)}, bf16[128,1024]{1,0:T(8,128)(2,1)S(1)}, u32[]{:S(2)}, u32[]{:S(2)}) collective-permute-start(bf16[128,1024]{1,0:T(8,128)(2,1)} %refs_0_.1), channel_id=1, source_target_pairs={{0,12},{2,14},{4,0},{6,2},{8,4},{10,6},{12,8},{14,10},{1,13},{3,15... | collective-permute-start | bytes 786440 | tf_op jit(solution)/shard_map/ppermute | solution.py:246
  9.1 2.8 %score.1 = (f32[16,8,128]{2,1,0:T(8,128)}, s32[128,1]{1,0:T(8,128)}) custom-call(bf16[128,1024]{1,0:T(8,128)(2,1)} %refs_0_.1, bf16[1024,1024]{1,0:T(8,128)(2,1)} %w1_ref.3, f32[1,1024]{1,0:T(1,128)} %bitcast.28, s32[1,128]{1,0:T(1,128)} %bitcast.30, s32[1,128]{1,0:T(1,128)} %bitcast.31, s32[1,128]{1,0:T(1,128)} %bitcast.32), custom_call_target="tpu_custom_call" | custom-call | tf_op jit(solution)/shard_map/score/pallas_call | solution.py:269
  11.9 43.7 %all-to-all-start = ((f32[16,8,128]{2,1,0:T(8,128)}), f32[16,8,128]{2,1,0:T(8,128)S(1)}, u32[]{:S(2)}, u32[]{:S(2)}) async-start(f32[16,8,128]{2,1,0:T(8,128)} %get-tuple-element.12), calls=%async_computation | async-start | bytes 131072 | tf_op jit(solution)/shard_map/all_to_all | solution.py:282
  55.7 4.0 %collective-permute-start.2 = (bf16[128,1024]{1,0:T(8,128)(2,1)S(1)}, bf16[128,1024]{1,0:T(8,128)(2,1)S(1)}, u32[]{:S(2)}, u32[]{:S(2)}) collective-permute-start(bf16[128,1024]{1,0:T(8,128)(2,1)S(1)} %broadcast_select_fusion), channel_id=1, source_target_pairs={{0,4},{1,13},{2,6},{3,15},{4,8},{5,1},{6,10},{7,3},{8,12},{9,5},{1... | collective-permute-start | bytes 786440 | tf_op jit(solution)/shard_map/ppermute | solution.py:255
  59.7 0.6 pad_add_fusion.place_ref
  60.2 7.9 %all-to-all-done.got_ref = f32[16,8,128]{2,1,0:T(8,128)S(1)} async-done(((f32[16,8,128]{2,1,0:T(8,128)}), f32[16,8,128]{2,1,0:T(8,128)S(1)}, u32[]{:S(2)}, u32[]{:S(2)}) %all-to-all-start) | async-done | bytes 65568 | tf_op jit(solution)/shard_map/all_to_all | solution.py:282
  68.1 4.1 %lambdas.1 = (f32[4,8,128]{2,1,0:T(8,128)}, f32[128,1]{1,0:T(8,128)}) custom-call(s32[3]{0:T(128)} %pad_add_fusion.place_ref, f32[16,8,128]{2,1,0:T(8,128)S(1)} %all-to-all-done.got_ref, s32[128,1]{1,0:T(8,128)} %get-tuple-element.13.slot_ref), custom_call_target="tpu_custom_call" | custom-call | tf_op jit(solution)/shard_map/lambdas/pallas_call | solution.py:283
  72.2 7.0 %all-to-all-start.1 = ((f32[4,8,128]{2,1,0:T(8,128)}), f32[4,8,128]{2,1,0:T(8,128)S(1)}, u32[]{:S(2)}, u32[]{:S(2)}) async-start(f32[4,8,128]{2,1,0:T(8,128)} %get-tuple-element.15), calls=%async_computation.1 | async-start | bytes 32768 | tf_op jit(solution)/shard_map/all_to_all | solution.py:293
  79.2 0.7 copy-done.3
  79.9 4.9 %slopes.1 = (bf16[4,128,1024]{2,1,0:T(8,128)(2,1)}, bf16[4,128,1024]{2,1,0:T(8,128)(2,1)}, bf16[4,128,256]{2,1,0:T(8,128)(2,1)}) custom-call(s32[3]{0:T(128)} %pad_add_fusion.place_ref, bf16[1024,1024]{1,0:T(8,128)(2,1)} %w1_ref.3, f32[1,1024]{1,0:T(1,128)} %bitcast.29, bf16[128,1024]{1,0:T(8,128)(2,1)} %refs_0_.1, bf16[128,1024]{1,0:T(8,128)(2,1)} %copy-done.1, ...), custom_call_target="tpu_custom_call" | custom-call | tf_op jit(solution)/shard_map/slopes/pallas_call | solution.py:186
  84.8 2.1 %all-to-all-done.1.lambda_ref = f32[4,8,128]{2,1,0:T(8,128)S(1)} async-done(((f32[4,8,128]{2,1,0:T(8,128)}), f32[4,8,128]{2,1,0:T(8,128)S(1)}, u32[]{:S(2)}, u32[]{:S(2)}) %all-to-all-start.1) | async-done | bytes 16416 | tf_op jit(solution)/shard_map/all_to_all | solution.py:293
  87.0 2.6 %product.1 = bf16[4,520,128]{2,1,0:T(8,128)(2,1)S(1)} custom-call(s32[3]{0:T(128)} %pad_add_fusion.place_ref, f32[4,8,128]{2,1,0:T(8,128)S(1)} %all-to-all-done.1.lambda_ref, bf16[4,128,1024]{2,1,0:T(8,128)(2,1)} %get-tuple-element.16.refs_0_, bf16[4,128,1024]{2,1,0:T(8,128)(2,1)} %get-tuple-element.17.refs_1_, bf16[4,128,256]{2,1,0:T(8,128)(2,1)} %get-tuple-element.18.refs_2_), custom_call_target="tpu_custom_call" | custom-call | tf_op jit(solution)/shard_map/product/pallas_call | solution.py:303
  89.6 0.0 copy-start
  89.6 11.5 %all_to_all.25 = bf16[4,520,128]{2,1,0:T(8,128)(2,1)S(1)} all-to-all(bf16[4,520,128]{2,1,0:T(8,128)(2,1)S(1)} %product.1), channel_id=1, replica_groups={{0,1,2,3},{4,5,6,7},{8,9,10,11},{12,13,14,15},{16,17,18,19},{20,21,22,2..., dimensions={0} | all-to-all | bytes 1064960 | tf_op jit(solution)/shard_map/all_to_all | solution.py:311
  101.1 0.1 reduce_sum.21
  101.3 17.9 %all_to_all.26 = bf16[16,40,128]{2,1,0:T(8,128)(2,1)S(1)} all-to-all(bf16[16,40,128]{2,1,0:T(8,128)(2,1)S(1)} %pad_maximum_fusion), channel_id=1, replica_groups=mesh['groups'=2,'docs'=16,'mp'=8,'sub'=2] {'docs'}, dimensions={0} | all-to-all | bytes 327680 | tf_op jit(solution)/shard_map/all_to_all | solution.py:318
  119.2 0.7 broadcast_in_dim.5
  119.9 5.4 %all-to-all-start.4 = ((bf16[16,32,128]{2,1,0:T(8,128)(2,1)}), bf16[16,32,128]{2,1,0:T(8,128)(2,1)S(1)}, u32[]{:S(2)}, u32[]{:S(2)}) async-start(bf16[16,32,128]{2,1,0:T(8,128)(2,1)} %broadcast_in_dim.5), calls=%async_computation.4 | async-start | bytes 262144 | tf_op jit(solution)/shard_map/all_to_all | solution.py:239
  125.3 0.1 reduce.1
  125.4 0.6 slice_bitcast_fusion
  126.1 2.5 %fusion = bf16[128,1024]{1,0:T(8,128)(2,1)} fusion(bf16[1024,1024]{1,0:T(8,128)(2,1)S(1)} %copy-done, bf16[4,128,1024]{2,1,0:T(8,128)(2,1)} %get-tuple-element.16.refs_0_, f32[128]{0:T(128)S(1)} %reduce.1), kind=kOutput, calls=%fused_computation.1 | convolution fusion | flops 268697600 | bytes 2621952 | tf_op jit(solution)/shard_map/dot_general | solution.py:321
  128.5 11.4 %all-to-all-done.4 = bf16[16,32,128]{2,1,0:T(8,128)(2,1)S(1)} async-done(((bf16[16,32,128]{2,1,0:T(8,128)(2,1)}), bf16[16,32,128]{2,1,0:T(8,128)(2,1)S(1)}, u32[]{:S(2)}, u32[]{:S(2)}) %all-to-all-start.4) | async-done | bytes 131104 | tf_op jit(solution)/shard_map/all_to_all | solution.py:239
  139.9 0.7 copy_bitcast_fusion
  (18 shorter events, 0.1 us)
Async XLA Ops:
  0.6 55.0 %collective-permute-start = (bf16[128,1024]{1,0:T(8,128)(2,1)}, bf16[128,1024]{1,0:T(8,128)(2,1)S(1)}, u32[]{:S(2)}, u32[]{:S(2)}) collective-permute-start(bf16[128,1024]{1,0:T(8,128)(2,1)} %refs_0_.1), channel_id=1, source_target_pairs={{0,4},{2,6},{4,8},{6,10},{8,12},{10,14},{12,0},{14,2},{1,5},{3,7},... | collective-permute-start | bytes 786440 | tf_op jit(solution)/shard_map/ppermute | solution.py:246
  5.3 50.4 %collective-permute-start.1 = (bf16[128,1024]{1,0:T(8,128)(2,1)}, bf16[128,1024]{1,0:T(8,128)(2,1)S(1)}, u32[]{:S(2)}, u32[]{:S(2)}) collective-permute-start(bf16[128,1024]{1,0:T(8,128)(2,1)} %refs_0_.1), channel_id=1, source_target_pairs={{0,12},{2,14},{4,0},{6,2},{8,4},{10,6},{12,8},{14,10},{1,13},{3,15... | collective-permute-start | bytes 786440 | tf_op jit(solution)/shard_map/ppermute | solution.py:246
  11.9 56.2 %all-to-all-start = ((f32[16,8,128]{2,1,0:T(8,128)}), f32[16,8,128]{2,1,0:T(8,128)S(1)}, u32[]{:S(2)}, u32[]{:S(2)}) async-start(f32[16,8,128]{2,1,0:T(8,128)} %get-tuple-element.12), calls=%async_computation | async-start | bytes 131072 | tf_op jit(solution)/shard_map/all_to_all | solution.py:282
  55.6 23.6 %copy-start.1 = (bf16[128,1024]{1,0:T(8,128)(2,1)}, bf16[128,1024]{1,0:T(8,128)(2,1)S(1)}, u32[]{:S(2)}) copy-start(bf16[128,1024]{1,0:T(8,128)(2,1)S(1)} %collective-permute-done.refs_1_) | copy-start | bytes 786436
  55.6 23.6 %copy-start.2 = (bf16[128,1024]{1,0:T(8,128)(2,1)}, bf16[128,1024]{1,0:T(8,128)(2,1)S(1)}, u32[]{:S(2)}) copy-start(bf16[128,1024]{1,0:T(8,128)(2,1)S(1)} %collective-permute-done.1.refs_2_) | copy-start | bytes 786436
  55.7 23.5 %collective-permute-start.2 = (bf16[128,1024]{1,0:T(8,128)(2,1)S(1)}, bf16[128,1024]{1,0:T(8,128)(2,1)S(1)}, u32[]{:S(2)}, u32[]{:S(2)}) collective-permute-start(bf16[128,1024]{1,0:T(8,128)(2,1)S(1)} %broadcast_select_fusion), channel_id=1, source_target_pairs={{0,4},{1,13},{2,6},{3,15},{4,8},{5,1},{6,10},{7,3},{8,12},{9,5},{1... | collective-permute-start | bytes 786440 | tf_op jit(solution)/shard_map/ppermute | solution.py:255
  72.2 14.8 %all-to-all-start.1 = ((f32[4,8,128]{2,1,0:T(8,128)}), f32[4,8,128]{2,1,0:T(8,128)S(1)}, u32[]{:S(2)}, u32[]{:S(2)}) async-start(f32[4,8,128]{2,1,0:T(8,128)} %get-tuple-element.15), calls=%async_computation.1 | async-start | bytes 32768 | tf_op jit(solution)/shard_map/all_to_all | solution.py:293
  79.2 0.7 copy-start.3
  89.6 35.7 %copy-start.4 = (f32[128,1]{1,0:T(8,128)S(1)}, f32[128,1]{1,0:T(8,128)}, u32[]{:S(2)}) copy-start(f32[128,1]{1,0:T(8,128)} %get-tuple-element.19) | copy-start | bytes 1540
  89.6 36.4 %copy-start = (bf16[1024,1024]{1,0:T(8,128)(2,1)S(1)}, bf16[1024,1024]{1,0:T(8,128)(2,1)}, u32[]{:S(2)}) copy-start(bf16[1024,1024]{1,0:T(8,128)(2,1)} %w1_ref.3) | copy-start | bytes 6291460
  119.9 20.0 %all-to-all-start.4 = ((bf16[16,32,128]{2,1,0:T(8,128)(2,1)}), bf16[16,32,128]{2,1,0:T(8,128)(2,1)S(1)}, u32[]{:S(2)}, u32[]{:S(2)}) async-start(bf16[16,32,128]{2,1,0:T(8,128)(2,1)} %broadcast_in_dim.5), calls=%async_computation.4 | async-start | bytes 262144 | tf_op jit(solution)/shard_map/all_to_all | solution.py:239
